TPU v7x, 128 devices: a whole 4x4x4 slice. The times are simulated.
128 devices in a mesh: dp: 1, sp: 128 (over z, y, x, core).
Axes of the slice: x: 4, y: 4, z: 4, core: 2. Of those that a mesh axis runs over, the one named last changes fastest.
Arguments:
- x_in: bfloat16 [65536, 512], P(('dp', 'sp'))
- w_q: bfloat16 [512, 512], replicated
- w_k: bfloat16 [512, 512], replicated
- w_v: bfloat16 [512, 512], replicated
- w_o: bfloat16 [512, 512], replicated
- dy_in: bfloat16 [65536, 512], P(('dp', 'sp'))
Outputs:
- output 1: bfloat16 [65536, 512], P(('dp', 'sp'))
- output 2: bfloat16 [65536, 512], P(('dp', 'sp'))
- output 3: float32 [512, 512], P('dp')
- output 4: float32 [512, 512], P('dp')
- output 5: float32 [512, 512], P('dp')
- output 6: float32 [512, 512], P('dp')
All inputs are finite; a program needn't handle non-finite values.
Results may differ from a plain program's by a relative error of at most 0.0120032.
Values are sent between devices in bfloat16 or wider.
A program may use at most 1 GiB of HBM per device.

v0:
```python
import functools

import jax
import jax.numpy as jnp
from jax import lax
from jax.experimental import pallas as pl
from jax.experimental.pallas import tpu as pltpu
from jax.sharding import PartitionSpec as P

HEAD_DIM = 64
F32 = jnp.float32
BF16 = jnp.bfloat16
MESH = pl.DeviceIdType.MESH
NN = (((1,), (0,)), ((), ()))
NT = (((1,), (1,)), ((), ()))
TN = (((0,), (0,)), ((), ()))


def dot(a, b, dims=NN):
    return lax.dot_general(a, b, dims, preferred_element_type=F32)


def two(ref, lead, start, n):
    return jnp.concatenate([ref[lead + (pl.ds(start, n), slice(None))], ref[lead + (pl.ds(256 + start, n), slice(None))]], axis=0)


def put_two(ref, lead, start, n, val):
    ref[lead + (pl.ds(start, n), slice(None))] = val[:n]
    ref[lead + (pl.ds(256 + start, n), slice(None))] = val[n:]


def wide(stat):
    return jnp.concatenate([stat, stat], axis=1)


def lanes_low(rows):
    return lax.broadcasted_iota(jnp.int32, (rows, 128), 1) < 64


def attention_kernel(x_ref, wq_ref, wk_ref, wv_ref, wo_ref, dy_ref, y_ref, dx_ref, dw_ref,
                     xp, dyp, qm, kt, vt, dom, g2, g3, est, ms, mh, lh, oh, lseh, delh, dqh, dka, dva, attnb, grads,
                     st2, st3, colt, rowt, s2s, s2r, s3s, s3r, t2s, t2r, t3s, t3r):
    me = lax.axis_index("sp")
    member = me % 4
    base = me - member
    peers = [None, base + (member + 1 - 2 * (member % 2)), base + (member + 2 - 4 * (member // 2)), base + 3 - member]

    barrier = pltpu.get_barrier_semaphore()
    for p in peers[1:]:
        pl.semaphore_signal(barrier, inc=1, device_id={"sp": p}, device_id_type=MESH)

    ri = lax.broadcasted_iota(jnp.int32, (256, 256), 0)
    ci = lax.broadcasted_iota(jnp.int32, (256, 256), 1)

    def token_of(i):
        blk = i >> 5
        return ((i & 31) << 3) + ((blk & 1) << 2) + (blk & 2) + (blk >> 2)

    one = jnp.ones((), F32)
    zero = jnp.zeros((), F32)
    perm = jnp.where(token_of(ri) == ci, one, zero).astype(BF16)
    for s in range(2):
        rows = slice(256 * s, 256 * s + 256)
        xp[rows, :] = dot(perm, x_ref[rows, :]).astype(BF16)
        dyp[rows, :] = dot(perm, dy_ref[rows, :]).astype(BF16)

    low = lanes_low(512)
    keep = [jnp.where(low, one, zero).astype(BF16), jnp.where(low, zero, one).astype(BF16)]

    for half in range(2):
        cols = slice(256 * half, 256 * half + 256)
        qq = dot(xp[...], wq_ref[:, cols]).astype(BF16) * jnp.asarray(HEAD_DIM ** -0.5, BF16)
        kk = dot(xp[...], wk_ref[:, cols]).astype(BF16)
        vv = dot(xp[...], wv_ref[:, cols]).astype(BF16)
        dd = dot(dyp[...], wo_ref[cols, :], NT).astype(BF16)
        for u in range(2):
            t = 2 * half + u
            lanes = slice(128 * u, 128 * u + 128)
            kt[t] = kk[:, lanes]
            vt[t] = vv[:, lanes]
            for par in range(2):
                qm[par, t] = qq[:, lanes] * keep[par]
                dom[par, t] = dd[:, lanes] * keep[par]
            for g, n, off in ((g2, 64, 64 * (t & 1)), (g3, 32, 32 * (2 * (t & 1) + (t >> 1)))):
                for a, ref in ((0, kk), (1, vv)):
                    for s in range(2):
                        r = 256 * s + off
                        g[a, t, n * s:n * s + n, :] = ref[r:r + n, lanes] * keep[0][:n] + ref[r + 128:r + 128 + n, lanes] * keep[1][:n]
                for a, ref in ((2, qq), (3, dd)):
                    for s in range(2):
                        r = 256 * s + off
                        g[a, t, n * s:n * s + n, :] = ref[r:r + n, lanes] * keep[0][:n] + ref[r + 128:r + 128 + n, lanes] * keep[1][:n]

    pl.semaphore_wait(barrier, 3)
    copies2 = []
    copies3 = []
    for a in range(4):
        c = pltpu.make_async_remote_copy(src_ref=g2.at[a, :, pl.ds(0, 128), :], dst_ref=g2.at[a, :, pl.ds(128, 128), :],
                                         send_sem=s2s.at[a], recv_sem=s2r.at[a], device_id={"sp": peers[1]}, device_id_type=MESH)
        c.start()
        copies2.append(c)
    for a in range(4):
        row = []
        for d in (2, 3, 1):
            c = pltpu.make_async_remote_copy(src_ref=g3.at[a, :, pl.ds(0, 64), :], dst_ref=g3.at[a, :, pl.ds(64 * d, 64), :],
                                             send_sem=s3s.at[a, d], recv_sem=s3r.at[a, d], device_id={"sp": peers[d]}, device_id_type=MESH)
            c.start()
            row.append(c)
        copies3.append(row)

    def forward(q, k, v):
        s = dot(q, k, NT)
        m = jnp.max(s, axis=1, keepdims=True)
        e = jnp.exp(s - m)
        l = jnp.sum(e, axis=1, keepdims=True)
        o = dot(e.astype(BF16), v)
        n = q.shape[0]
        return jnp.broadcast_to(m, (n, 128)), jnp.broadcast_to(l, (n, 128)), o, e

    def merge(t, par, start, n, m, l, o):
        m0 = two(mh, (t, par), start, n)
        l0 = two(lh, (t, par), start, n)
        o0 = two(oh, (t, par), start, n)
        mn = jnp.maximum(m0, m)
        a = jnp.exp(m0 - mn)
        b = jnp.exp(m - mn)
        put_two(mh, (t, par), start, n, mn)
        put_two(lh, (t, par), start, n, l0 * a + l * b)
        put_two(oh, (t, par), start, n, o0 * a + o * b)

    def off2(t, par):
        return pl.multiple_of(128 * par + 64 * (t % 2), 64)

    def off3(t, par):
        return pl.multiple_of(128 * par + 64 * (t % 2) + 32 * (t // 2), 32)

    def fwd_local(t, carry):
        for par in range(2):
            for s in range(2):
                rows = slice(256 * s, 256 * s + 256)
                m, l, o, e = forward(qm[par, t, rows, :], kt[t, rows, :], vt[t, rows, :])
                mh[t, par, rows, :] = m
                lh[t, par, rows, :] = l
                oh[t, par, rows, :] = o
                ms[t, par, rows, :] = m
                est[t, par, rows, :] = e
            m, l, o, e = forward(two(qm, (par, t), 128 * par, 128), two(kt, (t,), 128 * par, 128), two(vt, (t,), 128 * par, 128))
            ms[t, par, 512:768, :] = m
            est[t, par, 512:768, :] = e
            merge(t, par, 128 * par, 128, m, l, o)
        return carry

    lax.fori_loop(0, 4, fwd_local, 0)

    for a in range(2):
        copies2[a].wait_recv()
        for c in copies3[a]:
            c.wait_recv()

    low256 = lanes_low(256)
    colt[...] = jnp.zeros_like(colt)

    def fwd_group(t, carry):
        atts = []
        for par in range(2):
            o2 = off2(t, par)
            m, l, o, e = forward(two(qm, (par, t), o2, 64), g2[0, t], g2[1, t])
            ms[t, par, 768:896, :] = m
            est[t, par, 768:896, :] = e
            merge(t, par, o2, 64, m, l, o)
            o3 = off3(t, par)
            m, l, o, e = forward(two(qm, (par, t), o3, 32), g3[0, t], g3[1, t])
            ms[t, par, 896:960, :] = m
            est[t, par, 896:960, :] = e
            merge(t, par, o3, 32, m, l, o)
            lt = lh[t, par]
            att = oh[t, par] / lt
            lse = mh[t, par] + jnp.log(lt)
            delta = jnp.broadcast_to(jnp.sum(dom[par, t].astype(F32) * att, axis=1, keepdims=True), (512, 128))
            lseh[t, par] = lse
            delh[t, par] = delta
            atts.append(att)
            h = 2 * t + par
            lane = lax.broadcasted_iota(jnp.int32, (512, 128), 1)
            colt[0:512, :] = jnp.where(lane == h, lse, jnp.where(lane == h + 8, delta, colt[0:512, :]))
            l2 = two(lseh, (t, par), o2, 64)
            d2 = two(delh, (t, par), o2, 64)
            colt[512:640, :] = jnp.where(lane[:128] == h, l2, jnp.where(lane[:128] == h + 8, d2, colt[512:640, :]))
            l3 = two(lseh, (t, par), o3, 32)
            d3 = two(delh, (t, par), o3, 32)
            l3 = jnp.concatenate([l3, l3], axis=0)
            d3 = jnp.concatenate([d3, d3], axis=0)
            colt[640:768, :] = jnp.where(lane[:128] == h, l3, jnp.where(lane[:128] == h + 8, d3, colt[640:768, :]))
        attnb[:, pl.ds(pl.multiple_of(128 * t, 128), 128)] = jnp.where(low, atts[0], atts[1]).astype(BF16)
        return carry

    lax.fori_loop(0, 4, fwd_group, 0)

    st2[0] = jnp.transpose(colt[512:640, :])[:16]
    st3[0] = jnp.transpose(colt[640:768, :])[:16]
    for j in range(4):
        r = jnp.transpose(colt[128 * j:128 * j + 128, :])
        rowt[:, 128 * j:128 * j + 128] = r[:16]
    stat2 = pltpu.make_async_remote_copy(src_ref=st2.at[0], dst_ref=st2.at[1], send_sem=t2s, recv_sem=t2r,
                                         device_id={"sp": peers[1]}, device_id_type=MESH)
    stat2.start()
    stats3 = []
    for d in (2, 3, 1):
        c = pltpu.make_async_remote_copy(src_ref=st3.at[0], dst_ref=st3.at[d], send_sem=t3s.at[d], recv_sem=t3r.at[d],
                                         device_id={"sp": peers[d]}, device_id_type=MESH)
        c.start()
        stats3.append(c)

    yb = dot(attnb[...], wo_ref[...]).astype(BF16)
    for s in range(2):
        rows = slice(256 * s, 256 * s + 256)
        y_ref[rows, :] = dot(perm, yb[rows, :], TN).astype(BF16)
    dw_ref[3] = dot(attnb[...], dyp[...], TN)

    def grad_q(d_rows, k, v, e, delta):
        dp = dot(d_rows, v, NT)
        ds = (e * (dp - wide(delta))).astype(BF16)
        return dot(ds, k)

    def grad_kv(q, d_rows, k, v, lse_row, delta_row):
        st = dot(k, q, NT)
        pt = jnp.exp(st - lse_row)
        dpt = dot(v, d_rows, NT)
        dst = (pt * (dpt - delta_row)).astype(BF16)
        return dot(dst, q), dot(pt.astype(BF16), d_rows)

    def row_of(ref, lead, i):
        return ref[lead + (pl.ds(i, 1), slice(None))]

    def bwd_local(t, carry):
        for par in range(2):
            h = 2 * t + par
            lse_row = row_of(rowt, (), h)
            del_row = row_of(rowt, (), h + 8)
            for s in range(2):
                rows = slice(256 * s, 256 * s + 256)
                dr = dom[par, t, rows, :]
                kr = kt[t, rows, :]
                vr = vt[t, rows, :]
                lse = lseh[t, par, rows, :]
                dqj = grad_q(dr, kr, vr, est[t, par, rows, :], delh[t, par, rows, :])
                dqh[par, rows, :] = dqj * jnp.exp(ms[t, par, rows, :] - lse)
                gk, gv = grad_kv(qm[par, t, rows, :], dr, kr, vr, lse_row[:, rows], del_row[:, rows])
                if par == 0:
                    dka[t, rows, :] = gk
                    dva[t, rows, :] = gv
                else:
                    dka[t, rows, :] += gk
                    dva[t, rows, :] += gv
            a = 128 * par
            dr = two(dom, (par, t), a, 128)
            kr = two(kt, (t,), a, 128)
            vr = two(vt, (t,), a, 128)
            f = jnp.exp(ms[t, par, 512:768, :] - two(lseh, (t, par), a, 128))
            dqj = f * grad_q(dr, kr, vr, est[t, par, 512:768, :], two(delh, (t, par), a, 128))
            put_two(dqh, (par,), a, 128, two(dqh, (par,), a, 128) + dqj)
            lr = jnp.concatenate([lse_row[:, a:a + 128], lse_row[:, 256 + a:256 + a + 128]], axis=1)
            dlr = jnp.concatenate([del_row[:, a:a + 128], del_row[:, 256 + a:256 + a + 128]], axis=1)
            gk, gv = grad_kv(two(qm, (par, t), a, 128), dr, kr, vr, lr, dlr)
            put_two(dka, (t,), a, 128, two(dka, (t,), a, 128) + gk)
            put_two(dva, (t,), a, 128, two(dva, (t,), a, 128) + gv)
            for lo, n, off, g in ((768, 64, off2(t, par), g2), (896, 32, off3(t, par), g3)):
                f = jnp.exp(ms[t, par, lo:lo + 2 * n, :] - two(lseh, (t, par), off, n))
                dqj = f * grad_q(two(dom, (par, t), off, n), g[0, t], g[1, t], est[t, par, lo:lo + 2 * n, :], two(delh, (t, par), off, n))
                put_two(dqh, (par,), off, n, two(dqh, (par,), off, n) + dqj)
        dq = jnp.where(low, dqh[0], dqh[1]) * (HEAD_DIM ** -0.5)
        grads[0, :, pl.ds(pl.multiple_of(128 * t, 128), 128)] = dq.astype(BF16)
        return carry

    lax.fori_loop(0, 4, bwd_local, 0)

    stat2.wait_recv()
    for c in stats3:
        c.wait_recv()
    for a in (2, 3):
        copies2[a].wait_recv()
        for c in copies3[a]:
            c.wait_recv()

    keep256 = [keep[0][:256], keep[1][:256]]

    def bwd_group(t, carry):
        for par in range(2):
            h = 2 * t + par
            lr = jnp.concatenate([row_of(st2, (0,), h), row_of(st2, (1,), h)], axis=1)
            dlr = jnp.concatenate([row_of(st2, (0,), h + 8), row_of(st2, (1,), h + 8)], axis=1)
            off = off2(t, par)
            gk, gv = grad_kv(g2[2, t] * keep256[par], g2[3, t] * keep256[par], two(kt, (t,), off, 64), two(vt, (t,), off, 64), lr, dlr)
            put_two(dka, (t,), off, 64, two(dka, (t,), off, 64) + gk)
            put_two(dva, (t,), off, 64, two(dva, (t,), off, 64) + gv)
            lo = lax.broadcasted_iota(jnp.int32, (1, 128), 1) < 64
            lr = jnp.concatenate([jnp.where(lo, row_of(st3, (0,), h), row_of(st3, (1,), h)), jnp.where(lo, row_of(st3, (2,), h), row_of(st3, (3,), h))], axis=1)
            dlr = jnp.concatenate([jnp.where(lo, row_of(st3, (0,), h + 8), row_of(st3, (1,), h + 8)), jnp.where(lo, row_of(st3, (2,), h + 8), row_of(st3, (3,), h + 8))], axis=1)
            off = off3(t, par)
            gk, gv = grad_kv(g3[2, t] * keep256[par], g3[3, t] * keep256[par], two(kt, (t,), off, 32), two(vt, (t,), off, 32), lr, dlr)
            put_two(dka, (t,), off, 32, two(dka, (t,), off, 32) + gk)
            put_two(dva, (t,), off, 32, two(dva, (t,), off, 32) + gv)
        cols = pl.ds(pl.multiple_of(128 * t, 128), 128)
        grads[1, :, cols] = dka[t].astype(BF16)
        grads[2, :, cols] = dva[t].astype(BF16)
        return carry

    lax.fori_loop(0, 4, bwd_group, 0)

    dxb = (dot(grads[0], wq_ref[...], NT) + dot(grads[1], wk_ref[...], NT) + dot(grads[2], wv_ref[...], NT)).astype(BF16)
    for s in range(2):
        rows = slice(256 * s, 256 * s + 256)
        dx_ref[rows, :] = dot(perm, dxb[rows, :], TN).astype(BF16)
    for i in range(3):
        dw_ref[i] = dot(xp[...], grads[i], TN)

    for c in copies2:
        c.wait_send()
    for row in copies3:
        for c in row:
            c.wait_send()
    stat2.wait_send()
    for c in stats3:
        c.wait_send()


def attention(x_loc, w_q, w_k, w_v, w_o, dy_loc):
    vmem = pl.BlockSpec(memory_space=pltpu.VMEM)
    sem = pltpu.SemaphoreType.DMA
    return pl.pallas_call(
        attention_kernel,
        out_shape=[jax.ShapeDtypeStruct((512, 512), BF16), jax.ShapeDtypeStruct((512, 512), BF16), jax.ShapeDtypeStruct((4, 512, 512), F32)],
        in_specs=[vmem] * 6,
        out_specs=[vmem] * 3,
        scratch_shapes=[
            pltpu.VMEM((512, 512), BF16), pltpu.VMEM((512, 512), BF16),
            pltpu.VMEM((2, 4, 512, 128), BF16), pltpu.VMEM((4, 512, 128), BF16), pltpu.VMEM((4, 512, 128), BF16), pltpu.VMEM((2, 4, 512, 128), BF16),
            pltpu.VMEM((4, 4, 256, 128), BF16), pltpu.VMEM((4, 4, 256, 128), BF16),
            pltpu.VMEM((4, 2, 960, 256), F32), pltpu.VMEM((4, 2, 960, 128), F32),
            pltpu.VMEM((4, 2, 512, 128), F32), pltpu.VMEM((4, 2, 512, 128), F32), pltpu.VMEM((4, 2, 512, 128), F32),
            pltpu.VMEM((4, 2, 512, 128), F32), pltpu.VMEM((4, 2, 512, 128), F32),
            pltpu.VMEM((2, 512, 128), F32), pltpu.VMEM((4, 512, 128), F32), pltpu.VMEM((4, 512, 128), F32),
            pltpu.VMEM((512, 512), BF16), pltpu.VMEM((3, 512, 512), BF16),
            pltpu.VMEM((2, 16, 128), F32), pltpu.VMEM((4, 16, 128), F32), pltpu.VMEM((768, 128), F32), pltpu.VMEM((16, 512), F32),
            sem((4,)), sem((4,)), sem((4, 4)), sem((4, 4)), sem, sem, sem((4,)), sem((4,)),
        ],
        compiler_params=pltpu.CompilerParams(collective_id=0, has_side_effects=True, vmem_limit_bytes=60 * 2 ** 20),
        name="attention_step",
    )(x_loc, w_q, w_k, w_v, w_o, dy_loc)


def solution(mesh):
    def device_step(x_loc, w_q, w_k, w_v, w_o, dy_loc):
        y_loc, dx_loc, dws = attention(x_loc, w_q, w_k, w_v, w_o, dy_loc)
        dws = lax.psum(dws, "sp")
        return y_loc, dx_loc, dws[0], dws[1], dws[2], dws[3]

    row_spec = P(("dp", "sp"), None)
    full_spec = P(None, None)
    grad_spec = P("dp", None)
    return jax.shard_map(device_step, mesh=mesh, in_specs=(row_spec, full_spec, full_spec, full_spec, full_spec, row_spec),
                         out_specs=(row_spec, row_spec, grad_spec, grad_spec, grad_spec, grad_spec), check_vma=False)
```

profile of v0, /device:TPU:1, one launch (start us, length us, event | category | flops | bytes accessed | tf_op | source)
XLA Modules:
  0.0 215.2 jit_solution(10178950136851617827)
XLA Ops:
  7.2 0.0 all-reduce.2.cloned.1.call-start
  7.2 38.3 %attention_step.1 = (bf16[512,512]{1,0:T(8,128)(2,1)}, bf16[512,512]{1,0:T(8,128)(2,1)}, f32[4,512,512]{2,1,0:T(8,128)}) custom-call(bf16[512,512]{1,0:T(8,128)(2,1)} %x_ref.1, bf16[512,512]{1,0:T(8,128)(2,1)} %wq_ref.1, bf16[512,512]{1,0:T(8,128)(2,1)} %wk_ref.1, bf16[512,512]{1,0:T(8,128)(2,1)} %wv_ref.1, bf16[512,512]{1,0:T(8,128)(2,1)} %wo_ref.1, ...), custom_call_target="tpu_custom_call" | custom-call | tf_op jit(solution)/shard_map/attention_step/pallas_call | solution.py:330
  45.5 0.0 all-reduce.2.cloned.1.call-update
  45.5 0.0 copy-start.1
  45.5 0.0 copy-start
  45.6 157.0 %all-reduce.2.cloned.1.call-done = f32[4,512,512]{2,1,0:T(8,128)} async-done(((f32[4,512,512]{2,1,0:T(8,128)}), f32[4,512,512]{2,1,0:T(8,128)}) %all-reduce.2.cloned.1.call-update) | async-done | bytes 4194320 | tf_op jit(solution)/shard_map/psum | solution.py:355
  202.5 4.2 %slice_bitcast_fusion = (f32[512,512]{1,0:T(8,128)}, f32[512,512]{1,0:T(8,128)}, f32[512,512]{1,0:T(8,128)}, f32[512,512]{1,0:T(8,128)}) fusion(f32[4,512,512]{2,1,0:T(8,128)} %all-reduce.2.cloned.1.call-done), kind=kLoop, calls=%fused_computation | loop fusion | bytes 8388608 | tf_op jit(solution)/shard_map/squeeze | solution.py:356
  206.8 0.0 copy-done.1
  206.8 0.8 copy.15
  207.6 0.0 copy-done
  207.6 0.8 copy.16
Async XLA Ops:
  7.2 195.4 %all-reduce.2.cloned.1.call-start = ((), (), s32[]{:S(2)}) async-start(), calls=%async_computation | async-start | bytes 8388608 | tf_op jit(solution)/shard_map/psum | solution.py:355
  45.5 161.3 %copy-start.1 = (bf16[512,512]{1,0:T(8,128)(2,1)S(1)}, bf16[512,512]{1,0:T(8,128)(2,1)}, u32[]{:S(2)}) copy-start(bf16[512,512]{1,0:T(8,128)(2,1)} %get-tuple-element.22) | copy-start | bytes 1572868
  45.5 162.0 %copy-start = (bf16[512,512]{1,0:T(8,128)(2,1)S(1)}, bf16[512,512]{1,0:T(8,128)(2,1)}, u32[]{:S(2)}) copy-start(bf16[512,512]{1,0:T(8,128)(2,1)} %get-tuple-element.23) | copy-start | bytes 1572868
Sparse Core Ops, SparseCore 0:
  45.7 156.8 all-reduce.1
where the time goes:
time: 215 us
  waiting for transfers between devices  157 us (73%)
  Pallas kernels  38.3 us (18%)
  between operations  14.1 us (7%)
  local copies, waits for them, and re-layouts  5.84 us (3%)
    psum x1, waiting for transfers between devices, device_step(): dws = lax.psum(dws, 'sp')  157 us
    pallas_call x1, Pallas kernels, attention(): pl.pallas_call(attention_kernel, out_shape=[jax.ShapeDtypeStruct((512, 51...  38.3 us
  transfers between devices with their start and end apart: 1, of which 1 were waited for; matrix products, arithmetic and copies ran while one was open for 0% of the time, Pallas kernels for 0%

commit v1 on v0

v1 whole, which is shorter than its diff:
```python
import functools

import jax
import jax.numpy as jnp
from jax import lax
from jax.experimental import pallas as pl
from jax.experimental.pallas import tpu as pltpu
from jax.sharding import PartitionSpec as P

HEAD_DIM = 64
N4 = 4
N8 = 8
N16 = 16
N32 = 32
N64 = 64
N128 = 128
N256 = 256
N512 = 512
N640 = 640
N768 = 768
N896 = 896
N1024 = 1024
F32 = jnp.float32
BF16 = jnp.bfloat16
MESH = pl.DeviceIdType.MESH
NN = (((1,), (0,)), ((), ()))
NT = (((1,), (1,)), ((), ()))
TN = (((0,), (0,)), ((), ()))


def dot(a, b, dims=NN):
    return lax.dot_general(a, b, dims, preferred_element_type=F32)


def two(ref, lead, start, n):
    return jnp.concatenate([ref[lead + (pl.ds(start, n), slice(None))], ref[lead + (pl.ds(N256 + start, n), slice(None))]], axis=0)


def put_two(ref, lead, start, n, val):
    ref[lead + (pl.ds(start, n), slice(None))] = val[:n]
    ref[lead + (pl.ds(N256 + start, n), slice(None))] = val[n:]


def wide(stat):
    return jnp.concatenate([stat, stat], axis=1)


def lanes_low(rows):
    return lax.broadcasted_iota(jnp.int32, (rows, N128), 1) < N64


def attention_kernel(x_ref, wq_ref, wk_ref, wv_ref, wo_ref, dy_ref, y_ref, dx_ref, dw_ref,
                     xp, dyp, qm, kt, vt, dom, g2, g3, est, ms, mh, lh, oh, lseh, delh, dqh, dka, dva, attnb, grads,
                     st2, st3, colt, rowt, s2s, s2r, s3s, s3r, t2s, t2r, t3s, t3r):
    me = lax.axis_index("sp")
    member = me % N4
    base = me - member
    peers = [None, base + (member + 1 - 2 * (member % 2)), base + (member + 2 - N4 * (member // 2)), base + 3 - member]

    barrier = pltpu.get_barrier_semaphore()
    for p in peers[1:]:
        pl.semaphore_signal(barrier, inc=1, device_id={"sp": p}, device_id_type=MESH)

    ri = lax.broadcasted_iota(jnp.int32, (N256, N256), 0)
    ci = lax.broadcasted_iota(jnp.int32, (N256, N256), 1)

    def token_of(i):
        blk = i >> 5
        return ((i & 31) << 3) + ((blk & 1) << 2) + (blk & 2) + (blk >> 2)

    one = jnp.ones((), F32)
    zero = jnp.zeros((), F32)
    perm = jnp.where(token_of(ri) == ci, one, zero).astype(BF16)
    for s in range(2):
        rows = slice(N256 * s, N256 * s + N256)
        xp[rows, :] = dot(perm, x_ref[rows, :]).astype(BF16)
        dyp[rows, :] = dot(perm, dy_ref[rows, :]).astype(BF16)

    low = lanes_low(N512)
    keep = [jnp.where(low, one, zero).astype(BF16), jnp.where(low, zero, one).astype(BF16)]

    for half in range(2):
        cols = slice(N256 * half, N256 * half + N256)
        qq = dot(xp[...], wq_ref[:, cols]).astype(BF16) * jnp.asarray(HEAD_DIM ** -0.5, BF16)
        kk = dot(xp[...], wk_ref[:, cols]).astype(BF16)
        vv = dot(xp[...], wv_ref[:, cols]).astype(BF16)
        dd = dot(dyp[...], wo_ref[cols, :], NT).astype(BF16)
        for u in range(2):
            t = 2 * half + u
            lanes = slice(N128 * u, N128 * u + N128)
            kt[t] = kk[:, lanes]
            vt[t] = vv[:, lanes]
            for par in range(2):
                qm[par, t] = qq[:, lanes] * keep[par]
                dom[par, t] = dd[:, lanes] * keep[par]
            for g, n, off in ((g2, N64, N64 * (t & 1)), (g3, N32, N32 * (2 * (t & 1) + (t >> 1)))):
                for a, ref in ((0, kk), (1, vv)):
                    for s in range(2):
                        r = N256 * s + off
                        g[a, t, n * s:n * s + n, :] = ref[r:r + n, lanes] * keep[0][:n] + ref[r + N128:r + N128 + n, lanes] * keep[1][:n]
                for a, ref in ((2, qq), (3, dd)):
                    for s in range(2):
                        r = N256 * s + off
                        g[a, t, n * s:n * s + n, :] = ref[r:r + n, lanes] * keep[0][:n] + ref[r + N128:r + N128 + n, lanes] * keep[1][:n]

    pl.semaphore_wait(barrier, 3)
    copies2 = []
    copies3 = []
    for a in range(N4):
        c = pltpu.make_async_remote_copy(src_ref=g2.at[a, :, pl.ds(0, N128), :], dst_ref=g2.at[a, :, pl.ds(N128, N128), :],
                                         send_sem=s2s.at[a], recv_sem=s2r.at[a], device_id={"sp": peers[1]}, device_id_type=MESH)
        c.start()
        copies2.append(c)
    for a in range(N4):
        row = []
        for d in (2, 3, 1):
            c = pltpu.make_async_remote_copy(src_ref=g3.at[a, :, pl.ds(0, N64), :], dst_ref=g3.at[a, :, pl.ds(N64 * d, N64), :],
                                             send_sem=s3s.at[a, d], recv_sem=s3r.at[a, d], device_id={"sp": peers[d]}, device_id_type=MESH)
            c.start()
            row.append(c)
        copies3.append(row)

    def forward(q, k, v):
        s = dot(q, k, NT)
        m = jnp.max(s, axis=1, keepdims=True)
        e = jnp.exp(s - m)
        l = jnp.sum(e, axis=1, keepdims=True)
        o = dot(e.astype(BF16), v)
        n = q.shape[0]
        return jnp.broadcast_to(m, (n, N128)), jnp.broadcast_to(l, (n, N128)), o, e

    def merge(t, par, start, n, m, l, o):
        m0 = two(mh, (t, par), start, n)
        l0 = two(lh, (t, par), start, n)
        o0 = two(oh, (t, par), start, n)
        mn = jnp.maximum(m0, m)
        a = jnp.exp(m0 - mn)
        b = jnp.exp(m - mn)
        put_two(mh, (t, par), start, n, mn)
        put_two(lh, (t, par), start, n, l0 * a + l * b)
        put_two(oh, (t, par), start, n, o0 * a + o * b)

    def off2(t, par):
        return pl.multiple_of(N128 * par + N64 * (t % 2), N64)

    def off3(t, par):
        return pl.multiple_of(N128 * par + N64 * (t % 2) + N32 * (t // 2), N32)

    def fwd_local(t, carry):
        for par in range(2):
            for s in range(2):
                rows = slice(N256 * s, N256 * s + N256)
                m, l, o, e = forward(qm[par, t, rows, :], kt[t, rows, :], vt[t, rows, :])
                mh[t, par, rows, :] = m
                lh[t, par, rows, :] = l
                oh[t, par, rows, :] = o
                ms[t, par, rows, :] = m
                est[t, par, rows, :] = e
            m, l, o, e = forward(two(qm, (par, t), N128 * par, N128), two(kt, (t,), N128 * par, N128), two(vt, (t,), N128 * par, N128))
            ms[t, par, N512:N768, :] = m
            est[t, par, N512:N768, :] = e
            merge(t, par, N128 * par, N128, m, l, o)
        return carry

    lax.fori_loop(0, N4, fwd_local, 0)

    for a in range(2):
        copies2[a].wait_recv()
        for c in copies3[a]:
            c.wait_recv()

    low256 = lanes_low(N256)
    colt[...] = jnp.zeros_like(colt)

    def fwd_group(t, carry):
        atts = []
        for par in range(2):
            o2 = off2(t, par)
            m, l, o, e = forward(two(qm, (par, t), o2, N64), g2[0, t], g2[1, t])
            ms[t, par, N768:N896, :] = m
            est[t, par, N768:N896, :] = e
            merge(t, par, o2, N64, m, l, o)
            o3 = off3(t, par)
            m, l, o, e = forward(two(qm, (par, t), o3, N32), g3[0, t], g3[1, t])
            ms[t, par, N896:960, :] = m
            est[t, par, N896:960, :] = e
            merge(t, par, o3, N32, m, l, o)
            lt = lh[t, par]
            att = oh[t, par] / lt
            lse = mh[t, par] + jnp.log(lt)
            delta = jnp.broadcast_to(jnp.sum(dom[par, t].astype(F32) * att, axis=1, keepdims=True), (N512, N128))
            lseh[t, par] = lse
            delh[t, par] = delta
            atts.append(att)
            h = 2 * t + par
            lane = lax.broadcasted_iota(jnp.int32, (N512, N128), 1)
            colt[0:N512, :] = jnp.where(lane == h, lse, jnp.where(lane == h + N8, delta, colt[0:N512, :]))
            l2 = two(lseh, (t, par), o2, N64)
            d2 = two(delh, (t, par), o2, N64)
            colt[N512:N640, :] = jnp.where(lane[:N128] == h, l2, jnp.where(lane[:N128] == h + N8, d2, colt[N512:N640, :]))
            l3 = two(lseh, (t, par), o3, N32)
            d3 = two(delh, (t, par), o3, N32)
            l3 = jnp.concatenate([l3, l3], axis=0)
            d3 = jnp.concatenate([d3, d3], axis=0)
            colt[N640:N768, :] = jnp.where(lane[:N128] == h, l3, jnp.where(lane[:N128] == h + N8, d3, colt[N640:N768, :]))
        attnb[:, pl.ds(pl.multiple_of(N128 * t, N128), N128)] = jnp.where(low, atts[0], atts[1]).astype(BF16)
        return carry

    lax.fori_loop(0, N4, fwd_group, 0)

    st2[0] = jnp.transpose(colt[N512:N640, :])[:N16]
    st3[0] = jnp.transpose(colt[N640:N768, :])[:N16]
    for j in range(N4):
        r = jnp.transpose(colt[N128 * j:N128 * j + N128, :])
        rowt[:, N128 * j:N128 * j + N128] = r[:N16]
    stat2 = pltpu.make_async_remote_copy(src_ref=st2.at[0], dst_ref=st2.at[1], send_sem=t2s, recv_sem=t2r,
                                         device_id={"sp": peers[1]}, device_id_type=MESH)
    stat2.start()
    stats3 = []
    for d in (2, 3, 1):
        c = pltpu.make_async_remote_copy(src_ref=st3.at[0], dst_ref=st3.at[d], send_sem=t3s.at[d], recv_sem=t3r.at[d],
                                         device_id={"sp": peers[d]}, device_id_type=MESH)
        c.start()
        stats3.append(c)

    yb = dot(attnb[...], wo_ref[...]).astype(BF16)
    for s in range(2):
        rows = slice(N256 * s, N256 * s + N256)
        y_ref[rows, :] = dot(perm, yb[rows, :], TN).astype(BF16)
    for t in range(N4):
        g = dot(attnb[:, N128 * t:N128 * t + N128], dyp[...], TN)
        for j in range(N4):
            dw_ref[t, 1536 + N128 * j:1664 + N128 * j, :] = g[:, N128 * j:N128 * j + N128]

    def grad_q(d_rows, k, v, e, delta):
        dp = dot(d_rows, v, NT)
        ds = (e * (dp - wide(delta))).astype(BF16)
        return dot(ds, k)

    def grad_kv(q, d_rows, k, v, lse_row, delta_row):
        st = dot(k, q, NT)
        pt = jnp.exp(st - lse_row)
        dpt = dot(v, d_rows, NT)
        dst = (pt * (dpt - delta_row)).astype(BF16)
        return dot(dst, q), dot(pt.astype(BF16), d_rows)

    def row_of(ref, lead, i):
        return ref[lead + (pl.ds(i, 1), slice(None))]

    def bwd_local(t, carry):
        for par in range(2):
            h = 2 * t + par
            lse_row = row_of(rowt, (), h)
            del_row = row_of(rowt, (), h + N8)
            for s in range(2):
                rows = slice(N256 * s, N256 * s + N256)
                dr = dom[par, t, rows, :]
                kr = kt[t, rows, :]
                vr = vt[t, rows, :]
                lse = lseh[t, par, rows, :]
                dqj = grad_q(dr, kr, vr, est[t, par, rows, :], delh[t, par, rows, :])
                dqh[par, rows, :] = dqj * jnp.exp(ms[t, par, rows, :] - lse)
                gk, gv = grad_kv(qm[par, t, rows, :], dr, kr, vr, lse_row[:, rows], del_row[:, rows])
                if par == 0:
                    dka[t, rows, :] = gk
                    dva[t, rows, :] = gv
                else:
                    dka[t, rows, :] += gk
                    dva[t, rows, :] += gv
            a = N128 * par
            dr = two(dom, (par, t), a, N128)
            kr = two(kt, (t,), a, N128)
            vr = two(vt, (t,), a, N128)
            f = jnp.exp(ms[t, par, N512:N768, :] - two(lseh, (t, par), a, N128))
            dqj = f * grad_q(dr, kr, vr, est[t, par, N512:N768, :], two(delh, (t, par), a, N128))
            put_two(dqh, (par,), a, N128, two(dqh, (par,), a, N128) + dqj)
            lr = jnp.concatenate([lse_row[:, a:a + N128], lse_row[:, N256 + a:N256 + a + N128]], axis=1)
            dlr = jnp.concatenate([del_row[:, a:a + N128], del_row[:, N256 + a:N256 + a + N128]], axis=1)
            gk, gv = grad_kv(two(qm, (par, t), a, N128), dr, kr, vr, lr, dlr)
            put_two(dka, (t,), a, N128, two(dka, (t,), a, N128) + gk)
            put_two(dva, (t,), a, N128, two(dva, (t,), a, N128) + gv)
            for lo, n, off, g in ((N768, N64, off2(t, par), g2), (N896, N32, off3(t, par), g3)):
                f = jnp.exp(ms[t, par, lo:lo + 2 * n, :] - two(lseh, (t, par), off, n))
                dqj = f * grad_q(two(dom, (par, t), off, n), g[0, t], g[1, t], est[t, par, lo:lo + 2 * n, :], two(delh, (t, par), off, n))
                put_two(dqh, (par,), off, n, two(dqh, (par,), off, n) + dqj)
        dq = jnp.where(low, dqh[0], dqh[1]) * (HEAD_DIM ** -0.5)
        grads[0, :, pl.ds(pl.multiple_of(N128 * t, N128), N128)] = dq.astype(BF16)
        return carry

    lax.fori_loop(0, N4, bwd_local, 0)

    stat2.wait_recv()
    for c in stats3:
        c.wait_recv()
    for a in (2, 3):
        copies2[a].wait_recv()
        for c in copies3[a]:
            c.wait_recv()

    keep256 = [keep[0][:N256], keep[1][:N256]]

    def bwd_group(t, carry):
        for par in range(2):
            h = 2 * t + par
            lr = jnp.concatenate([row_of(st2, (0,), h), row_of(st2, (1,), h)], axis=1)
            dlr = jnp.concatenate([row_of(st2, (0,), h + N8), row_of(st2, (1,), h + N8)], axis=1)
            off = off2(t, par)
            gk, gv = grad_kv(g2[2, t] * keep256[par], g2[3, t] * keep256[par], two(kt, (t,), off, N64), two(vt, (t,), off, N64), lr, dlr)
            put_two(dka, (t,), off, N64, two(dka, (t,), off, N64) + gk)
            put_two(dva, (t,), off, N64, two(dva, (t,), off, N64) + gv)
            lo = lax.broadcasted_iota(jnp.int32, (1, N128), 1) < N64
            lr = jnp.concatenate([jnp.where(lo, row_of(st3, (0,), h), row_of(st3, (1,), h)), jnp.where(lo, row_of(st3, (2,), h), row_of(st3, (3,), h))], axis=1)
            dlr = jnp.concatenate([jnp.where(lo, row_of(st3, (0,), h + N8), row_of(st3, (1,), h + N8)), jnp.where(lo, row_of(st3, (2,), h + N8), row_of(st3, (3,), h + N8))], axis=1)
            off = off3(t, par)
            gk, gv = grad_kv(g3[2, t] * keep256[par], g3[3, t] * keep256[par], two(kt, (t,), off, N32), two(vt, (t,), off, N32), lr, dlr)
            put_two(dka, (t,), off, N32, two(dka, (t,), off, N32) + gk)
            put_two(dva, (t,), off, N32, two(dva, (t,), off, N32) + gv)
        cols = pl.ds(pl.multiple_of(N128 * t, N128), N128)
        grads[1, :, cols] = dka[t].astype(BF16)
        grads[2, :, cols] = dva[t].astype(BF16)
        return carry

    lax.fori_loop(0, N4, bwd_group, 0)

    dxb = (dot(grads[0], wq_ref[...], NT) + dot(grads[1], wk_ref[...], NT) + dot(grads[2], wv_ref[...], NT)).astype(BF16)
    for s in range(2):
        rows = slice(N256 * s, N256 * s + N256)
        dx_ref[rows, :] = dot(perm, dxb[rows, :], TN).astype(BF16)
    for i in range(3):
        g = dot(xp[...], grads[i], TN)
        for t in range(N4):
            dw_ref[t, N512 * i:N512 * i + N512, :] = g[:, N128 * t:N128 * t + N128]

    for c in copies2:
        c.wait_send()
    for row in copies3:
        for c in row:
            c.wait_send()
    stat2.wait_send()
    for c in stats3:
        c.wait_send()


def attention(x_loc, w_q, w_k, w_v, w_o, dy_loc):
    vmem = pl.BlockSpec(memory_space=pltpu.VMEM)
    sem = pltpu.SemaphoreType.DMA
    return pl.pallas_call(
        attention_kernel,
        out_shape=[jax.ShapeDtypeStruct((N512, N512), BF16), jax.ShapeDtypeStruct((N512, N512), BF16), jax.ShapeDtypeStruct((N4, 2048, N128), F32)],
        in_specs=[vmem] * 6,
        out_specs=[vmem] * 3,
        scratch_shapes=[
            pltpu.VMEM((N512, N512), BF16), pltpu.VMEM((N512, N512), BF16),
            pltpu.VMEM((2, N4, N512, N128), BF16), pltpu.VMEM((N4, N512, N128), BF16), pltpu.VMEM((N4, N512, N128), BF16), pltpu.VMEM((2, N4, N512, N128), BF16),
            pltpu.VMEM((N4, N4, N256, N128), BF16), pltpu.VMEM((N4, N4, N256, N128), BF16),
            pltpu.VMEM((N4, 2, 960, N256), F32), pltpu.VMEM((N4, 2, 960, N128), F32),
            pltpu.VMEM((N4, 2, N512, N128), F32), pltpu.VMEM((N4, 2, N512, N128), F32), pltpu.VMEM((N4, 2, N512, N128), F32),
            pltpu.VMEM((N4, 2, N512, N128), F32), pltpu.VMEM((N4, 2, N512, N128), F32),
            pltpu.VMEM((2, N512, N128), F32), pltpu.VMEM((N4, N512, N128), F32), pltpu.VMEM((N4, N512, N128), F32),
            pltpu.VMEM((N512, N512), BF16), pltpu.VMEM((3, N512, N512), BF16),
            pltpu.VMEM((2, N16, N128), F32), pltpu.VMEM((N4, N16, N128), F32), pltpu.VMEM((N768, N128), F32), pltpu.VMEM((N16, N512), F32),
            sem((N4,)), sem((N4,)), sem((N4, N4)), sem((N4, N4)), sem, sem, sem((N4,)), sem((N4,)),
        ],
        compiler_params=pltpu.CompilerParams(collective_id=0, has_side_effects=True, vmem_limit_bytes=60 * 2 ** 20),
        name="attention_step",
    )(x_loc, w_q, w_k, w_v, w_o, dy_loc)


COLOR_ROWS = (384, 384, N256)
COLOR_BASE = (0, 384, N768)
STRIDES = (2, N8, N32)


class Reducer:
    def __init__(self, cb, res, pbuf, r1, r2, r3, sems):
        self.cb, self.res, self.pbuf, self.r1, self.r2, self.r3 = cb, res, pbuf, r1, r2, r3
        (self.p0s, self.p0r, self.p1s, self.p1r, self.p2s, self.p2r, self.p3s, self.p3r,
         self.p4s, self.p4r, self.p5s, self.p5r, self.p6s, self.p6r) = sems
        self.me = lax.axis_index("sp")
        self.core = self.me % 2
        self.coord = [(self.me // s) % N4 for s in STRIDES]
        self.mate = self.me + 1 - 2 * self.core

    def peer(self, axis, d):
        return self.me + STRIDES[axis] * ((self.coord[axis] + d) % N4 - self.coord[axis])

    def send(self, src, dst, ss, rs, dev):
        return pltpu.make_async_remote_copy(src_ref=src, dst_ref=dst, send_sem=ss, recv_sem=rs, device_id={"sp": dev}, device_id_type=MESH)

    def half(self, core):
        return pl.ds(pl.multiple_of(N1024 * core, N1024), N1024)

    def rows(self, k, q, p=None):
        n = COLOR_ROWS[k]
        start = N1024 * self.core + COLOR_BASE[k] + (n // N4) * q
        if p is None:
            return pl.ds(pl.multiple_of(start, N8), n // N4)
        return pl.ds(pl.multiple_of(start + (n // N16) * p, N8), n // N16)

    def c0(self, c):
        return self.send(self.cb.at[c, self.half(1 - self.core)], self.pbuf.at[c], self.p0s.at[c], self.p0r.at[c], self.mate)

    def c1(self, c, k, d):
        n = COLOR_ROWS[k] // N4
        a = self.coord[k]
        return self.send(self.cb.at[c, self.rows(k, (a + d) % N4)], self.r1.at[c, k, a, pl.ds(0, n)], self.p1s.at[c, k, d], self.p1r.at[c, k, d], self.peer(k, d))

    def c2(self, c, k, d):
        n = COLOR_ROWS[k] // N16
        b = (k + 1) % 3
        a = self.coord[b]
        src = self.cb.at[c, self.rows(k, self.coord[k], (a + d) % N4)]
        return self.send(src, self.r2.at[c, k, a, pl.ds(0, n)], self.p2s.at[c, k, d], self.p2r.at[c, k, d], self.peer(b, d))

    def c3(self, c, k, d):
        n = COLOR_ROWS[k] // N16
        b = (k + 2) % 3
        a = self.coord[b]
        src = self.cb.at[c, self.rows(k, self.coord[k], self.coord[(k + 1) % 3])]
        return self.send(src, self.r3.at[c, k, a, pl.ds(0, n)], self.p3s.at[c, k, d], self.p3r.at[c, k, d], self.peer(b, d))

    def c4(self, c, k, d):
        b = (k + 1) % 3
        part = self.res.at[c, self.rows(k, self.coord[k], self.coord[b])]
        return self.send(part, part, self.p4s.at[c, k, d], self.p4r.at[c, k, d], self.peer(b, d))

    def c5(self, c, k, d):
        part = self.res.at[c, self.rows(k, self.coord[k])]
        return self.send(part, part, self.p5s.at[c, k, d], self.p5r.at[c, k, d], self.peer(k, d))

    def c6(self, c):
        part = self.res.at[c, self.half(self.core)]
        return self.send(part, part, self.p6s.at[c], self.p6r.at[c], self.mate)

    def each(self, make, c):
        return [make(c, k, d) for d in (1, 3, 2) for k in range(3)]

    def phase(self, i, c):
        core = self.core
        if i == 0:
            self.c0(c).start()
        elif i == 1:
            self.c0(c).wait_recv()
            mine = self.half(core)
            self.cb[c, mine, :] = self.cb[c, mine, :] + self.pbuf[c]
            for x in self.each(self.c1, c):
                x.start()
        elif i == 2:
            for k in range(3):
                for d in (1, 3, 2):
                    self.c1(c, k, d).wait_recv()
                self.total(c, k, self.r1, self.rows(k, self.coord[k]), self.coord[k], COLOR_ROWS[k] // N4, self.cb)
                for d in (1, 3, 2):
                    self.c2(c, k, d).start()
        elif i == 3:
            for k in range(3):
                for d in (1, 3, 2):
                    self.c2(c, k, d).wait_recv()
                b = (k + 1) % 3
                self.total(c, k, self.r2, self.rows(k, self.coord[k], self.coord[b]), self.coord[b], COLOR_ROWS[k] // N16, self.cb)
                for d in (1, 3, 2):
                    self.c3(c, k, d).start()
        elif i == N4:
            for k in range(3):
                for d in (1, 3, 2):
                    self.c3(c, k, d).wait_recv()
                b = (k + 2) % 3
                self.total(c, k, self.r3, self.rows(k, self.coord[k], self.coord[(k + 1) % 3]), self.coord[b], COLOR_ROWS[k] // N16, self.res)
                for d in (1, 3, 2):
                    self.c4(c, k, d).start()
        elif i == 5:
            for k in range(3):
                for d in (1, 3, 2):
                    self.c4(c, k, d).wait_recv()
                for d in (1, 3, 2):
                    self.c5(c, k, d).start()
        elif i == 6:
            for k in range(3):
                for d in (1, 3, 2):
                    self.c5(c, k, d).wait_recv()
            self.c6(c).start()
        elif i == 7:
            self.c6(c).wait_recv()

    def total(self, c, k, slots, rows, a, n, out):
        slots[c, k, a, 0:n, :] = self.cb[c, rows, :]
        out[c, rows, :] = (slots[c, k, 0, 0:n, :] + slots[c, k, 1, 0:n, :]) + (slots[c, k, 2, 0:n, :] + slots[c, k, 3, 0:n, :])

    def finish(self, c):
        self.c0(c).wait_send()
        for make in (self.c1, self.c2, self.c3, self.c4, self.c5):
            for x in self.each(make, c):
                x.wait_send()
        self.c6(c).wait_send()


def reducer_scratch():
    sem = pltpu.SemaphoreType.DMA
    bufs = [pltpu.VMEM((N4, 2048, N128), F32), pltpu.VMEM((N4, N1024, N128), F32), pltpu.VMEM((N4, 3, N4, 96, N128), F32),
            pltpu.VMEM((N4, 3, N4, 24, N128), F32), pltpu.VMEM((N4, 3, N4, 24, N128), F32)]
    sems = [sem((N4,)), sem((N4,))] + [sem((N4, 3, N4))] * 10 + [sem((N4,)), sem((N4,))]
    return bufs, sems


def write_out(res, outs, sem, t):
    copies = []
    cols = pl.ds(pl.multiple_of(N128 * t, N128), N128)
    for i in range(3):
        copies.append(pltpu.make_async_copy(res.at[t, pl.ds(N512 * i, N512)], outs[i].at[:, cols], sem.at[t, i]))
    for j in range(N4):
        copies.append(pltpu.make_async_copy(res.at[t, pl.ds(1536 + N128 * j, N128)], outs[3].at[cols, pl.ds(N128 * j, N128)], sem.at[t, 3 + j]))
    return copies


def reduce_kernel(cb, o0, o1, o2, o3, work, res, pbuf, r1, r2, r3, wsem, *sems):
    red = Reducer(work, res, pbuf, r1, r2, r3, sems)
    barrier = pltpu.get_barrier_semaphore()
    peers = [red.mate] + [red.peer(a, d) for a in range(3) for d in (1, 2, 3)]
    for p in peers:
        pl.semaphore_signal(barrier, inc=1, device_id={"sp": p}, device_id_type=MESH)
    work[...] = cb[...]
    pl.semaphore_wait(barrier, len(peers))
    for i in range(N8):
        for c in range(N4):
            red.phase(i, c)
            if i == 7:
                for x in write_out(res, (o0, o1, o2, o3), wsem, c):
                    x.start()
    for c in range(N4):
        red.finish(c)
        for x in write_out(res, (o0, o1, o2, o3), wsem, c):
            x.wait()


def reduce_grads(chunks):
    vmem = pl.BlockSpec(memory_space=pltpu.VMEM)
    bufs, sems = reducer_scratch()
    return pl.pallas_call(
        reduce_kernel,
        out_shape=[jax.ShapeDtypeStruct((N512, N512), F32)] * N4,
        in_specs=[vmem],
        out_specs=[pl.BlockSpec(memory_space=pl.ANY)] * N4,
        scratch_shapes=[pltpu.VMEM((N4, 2048, N128), F32)] + bufs + [pltpu.SemaphoreType.DMA((N4, 7))] + sems,
        compiler_params=pltpu.CompilerParams(collective_id=1, has_side_effects=True, vmem_limit_bytes=60 * 2 ** 20),
        name="reduce_grads",
    )(chunks)


def solution(mesh):
    def device_step(x_loc, w_q, w_k, w_v, w_o, dy_loc):
        y_loc, dx_loc, dws = attention(x_loc, w_q, w_k, w_v, w_o, dy_loc)
        return y_loc, dx_loc, *reduce_grads(dws)

    row_spec = P(("dp", "sp"), None)
    full_spec = P(None, None)
    grad_spec = P("dp", None)
    return jax.shard_map(device_step, mesh=mesh, in_specs=(row_spec, full_spec, full_spec, full_spec, full_spec, row_spec),
                         out_specs=(row_spec, row_spec, grad_spec, grad_spec, grad_spec, grad_spec), check_vma=False)
```

time: 215 us -> 91.3 us (0.42)
  waiting for transfers between devices: 157 us -> 0 us
  Pallas kernels: 38.3 us -> 83.7 us
  between operations: 14.1 us -> 0.7 us
    psum x1 -> x0, waiting for transfers between devices: 157 us -> none  [device_step(): dws = lax.psum(dws, 'sp')]
    pallas_call x1 -> x2, Pallas kernels: 38.3 us -> 83.7 us  [the longest x1 45.4 us: reduce_grads(): pl.pallas_call(reduce_kernel, out_shape=[jax.ShapeDtypeStruct((N512, N512...]
    unnamed x6 -> x16, local copies, waits for them, and re-layouts: 1.59 us -> 6.78 us
    squeeze x1 -> x0, local copies, waits for them, and re-layouts: 4.25 us -> none  [device_step(): return (y_loc, dx_loc, dws[0], dws[1], dws[2], dws[3])]
  transfers between devices with their start and end apart: 1 -> 0, of which waited for: 1 -> 0; matrix products, arithmetic and copies ran while one was open for 0% -> 0% of each run, Pallas kernels for 0% -> 0%
where the time goes in v1:
time: 91.3 us; the launch traced here: 91.2 us
  Pallas kernels  83.7 us (92%)
  local copies, waits for them, and re-layouts  6.78 us (7%)
    pallas_call x1, Pallas kernels, reduce_grads(): pl.pallas_call(reduce_kernel, out_shape=[jax.ShapeDtypeStruct((N512, N512...  45.4 us
    pallas_call x1, Pallas kernels, attention(): pl.pallas_call(attention_kernel, out_shape=[jax.ShapeDtypeStruct((N512, N...  38.3 us
    unnamed x16, local copies, waits for them, and re-layouts  6.78 us

profile of v1, /device:TPU:1, one launch (start us, length us, event | category | flops | bytes accessed | tf_op | source)
XLA Modules:
  0.0 91.2 jit_solution(8515098363672778868)
XLA Ops:
  0.6 38.3 %attention_step.1 = (bf16[512,512]{1,0:T(8,128)(2,1)}, bf16[512,512]{1,0:T(8,128)(2,1)}, f32[4,2048,128]{2,1,0:T(8,128)}) custom-call(bf16[512,512]{1,0:T(8,128)(2,1)} %x_ref.1, bf16[512,512]{1,0:T(8,128)(2,1)} %wq_ref.1, bf16[512,512]{1,0:T(8,128)(2,1)} %wk_ref.1, bf16[512,512]{1,0:T(8,128)(2,1)} %wv_ref.1, bf16[512,512]{1,0:T(8,128)(2,1)} %wo_ref.1, ...), custom_call_target="tpu_custom_call" | custom-call | tf_op jit(solution)/shard_map/attention_step/pallas_call | solution.py:347
  38.9 0.0 copy-start.4
  38.9 0.0 copy-start.3
  38.9 45.4 %reduce_grads.1 = (f32[512,512]{1,0:T(8,128)}, f32[512,512]{1,0:T(8,128)}, f32[512,512]{1,0:T(8,128)}, f32[512,512]{1,0:T(8,128)}) custom-call(f32[4,2048,128]{2,1,0:T(8,128)} %get-tuple-element.15.cb), custom_call_target="tpu_custom_call" | custom-call | tf_op jit(solution)/shard_map/reduce_grads/pallas_call | solution.py:538
  84.4 0.0 copy-start.2
  84.4 0.0 copy-start.1
  84.4 0.0 copy-done.4
  84.4 0.0 copy-start
  84.4 0.8 copy.18
  85.2 0.0 copy-done.3
  85.2 0.8 copy.19
  86.0 2.3 %copy.20 = f32[512,512]{1,0:T(8,128)} copy(f32[512,512]{1,0:T(8,128)} %get-tuple-element.28) | data formatting | bytes 2097152
  88.3 0.0 copy-done.2
  88.3 1.0 %copy.21 = f32[512,512]{1,0:T(8,128)} copy(f32[512,512]{1,0:T(8,128)S(1)} %copy-done.2) | data formatting | bytes 2097152
  89.2 0.0 copy-done.1
  89.2 1.0 %copy.22 = f32[512,512]{1,0:T(8,128)} copy(f32[512,512]{1,0:T(8,128)S(1)} %copy-done.1) | data formatting | bytes 2097152
  90.2 0.0 copy-done
  90.2 1.0 %copy.23 = f32[512,512]{1,0:T(8,128)} copy(f32[512,512]{1,0:T(8,128)S(1)} %copy-done) | data formatting | bytes 2097152
Async XLA Ops:
  38.9 45.5 %copy-start.4 = (bf16[512,512]{1,0:T(8,128)(2,1)S(1)}, bf16[512,512]{1,0:T(8,128)(2,1)}, u32[]{:S(2)}) copy-start(bf16[512,512]{1,0:T(8,128)(2,1)} %get-tuple-element.26) | copy-start | bytes 1572868
  38.9 46.3 %copy-start.3 = (bf16[512,512]{1,0:T(8,128)(2,1)S(1)}, bf16[512,512]{1,0:T(8,128)(2,1)}, u32[]{:S(2)}) copy-start(bf16[512,512]{1,0:T(8,128)(2,1)} %get-tuple-element.27) | copy-start | bytes 1572868
  84.4 3.9 %copy-start.2 = (f32[512,512]{1,0:T(8,128)S(1)}, f32[512,512]{1,0:T(8,128)}, u32[]{:S(2)}) copy-start(f32[512,512]{1,0:T(8,128)} %get-tuple-element.29) | copy-start | bytes 3145732
  84.4 4.9 %copy-start.1 = (f32[512,512]{1,0:T(8,128)S(1)}, f32[512,512]{1,0:T(8,128)}, u32[]{:S(2)}) copy-start(f32[512,512]{1,0:T(8,128)} %get-tuple-element.30) | copy-start | bytes 3145732
  84.4 5.8 %copy-start = (f32[512,512]{1,0:T(8,128)S(1)}, f32[512,512]{1,0:T(8,128)}, u32[]{:S(2)}) copy-start(f32[512,512]{1,0:T(8,128)} %get-tuple-element.31) | copy-start | bytes 3145732

commit v2 on v0

v2 whole, which is shorter than its diff:
```python
import functools

import jax
import jax.numpy as jnp
from jax import lax
from jax.experimental import pallas as pl
from jax.experimental.pallas import tpu as pltpu
from jax.sharding import PartitionSpec as P

HEAD_DIM = 64
N4 = 4
N8 = 8
N16 = 16
N32 = 32
N64 = 64
N128 = 128
N256 = 256
N512 = 512
N640 = 640
N768 = 768
N896 = 896
N1024 = 1024
F32 = jnp.float32
BF16 = jnp.bfloat16
MESH = pl.DeviceIdType.MESH
NN = (((1,), (0,)), ((), ()))
NT = (((1,), (1,)), ((), ()))
TN = (((0,), (0,)), ((), ()))


def dot(a, b, dims=NN):
    return lax.dot_general(a, b, dims, preferred_element_type=F32)


def two(ref, lead, start, n):
    return jnp.concatenate([ref[lead + (pl.ds(start, n), slice(None))], ref[lead + (pl.ds(N256 + start, n), slice(None))]], axis=0)


def put_two(ref, lead, start, n, val):
    ref[lead + (pl.ds(start, n), slice(None))] = val[:n]
    ref[lead + (pl.ds(N256 + start, n), slice(None))] = val[n:]


def wide(stat):
    return jnp.concatenate([stat, stat], axis=1)


def lanes_low(rows):
    return lax.broadcasted_iota(jnp.int32, (rows, N128), 1) < N64


COLOR_ROWS = (384, 384, N256)
COLOR_BASE = (0, 384, N768)
STRIDES = (2, N8, N32)


class Reducer:
    def __init__(self, cb, res, pbuf, r1, r2, r3, sems):
        self.cb, self.res, self.pbuf, self.r1, self.r2, self.r3 = cb, res, pbuf, r1, r2, r3
        (self.p0s, self.p0r, self.p1s, self.p1r, self.p2s, self.p2r, self.p3s, self.p3r,
         self.p4s, self.p4r, self.p5s, self.p5r, self.p6s, self.p6r) = sems
        self.me = lax.axis_index("sp")
        self.core = self.me % 2
        self.coord = [(self.me // s) % N4 for s in STRIDES]
        self.mate = self.me + 1 - 2 * self.core

    def peer(self, axis, d):
        return self.me + STRIDES[axis] * ((self.coord[axis] + d) % N4 - self.coord[axis])

    def send(self, src, dst, ss, rs, dev):
        return pltpu.make_async_remote_copy(src_ref=src, dst_ref=dst, send_sem=ss, recv_sem=rs, device_id={"sp": dev}, device_id_type=MESH)

    def half(self, core):
        return pl.ds(pl.multiple_of(N1024 * core, N1024), N1024)

    def rows(self, k, q, p=None):
        n = COLOR_ROWS[k]
        start = N1024 * self.core + COLOR_BASE[k] + (n // N4) * q
        if p is None:
            return pl.ds(pl.multiple_of(start, N8), n // N4)
        return pl.ds(pl.multiple_of(start + (n // N16) * p, N8), n // N16)

    def c0(self, c):
        return self.send(self.cb.at[c, self.half(1 - self.core)], self.pbuf.at[c], self.p0s.at[c], self.p0r.at[c], self.mate)

    def c1(self, c, k, d):
        n = COLOR_ROWS[k] // N4
        a = self.coord[k]
        return self.send(self.cb.at[c, self.rows(k, (a + d) % N4)], self.r1.at[c, k, a, pl.ds(0, n)], self.p1s.at[c, k, d], self.p1r.at[c, k, d], self.peer(k, d))

    def c2(self, c, k, d):
        n = COLOR_ROWS[k] // N16
        b = (k + 1) % 3
        a = self.coord[b]
        src = self.cb.at[c, self.rows(k, self.coord[k], (a + d) % N4)]
        return self.send(src, self.r2.at[c, k, a, pl.ds(0, n)], self.p2s.at[c, k, d], self.p2r.at[c, k, d], self.peer(b, d))

    def c3(self, c, k, d):
        n = COLOR_ROWS[k] // N16
        b = (k + 2) % 3
        a = self.coord[b]
        src = self.cb.at[c, self.rows(k, self.coord[k], self.coord[(k + 1) % 3])]
        return self.send(src, self.r3.at[c, k, a, pl.ds(0, n)], self.p3s.at[c, k, d], self.p3r.at[c, k, d], self.peer(b, d))

    def c4(self, c, k, d):
        b = (k + 1) % 3
        part = self.res.at[c, self.rows(k, self.coord[k], self.coord[b])]
        return self.send(part, part, self.p4s.at[c, k, d], self.p4r.at[c, k, d], self.peer(b, d))

    def c5(self, c, k, d):
        part = self.res.at[c, self.rows(k, self.coord[k])]
        return self.send(part, part, self.p5s.at[c, k, d], self.p5r.at[c, k, d], self.peer(k, d))

    def c6(self, c):
        part = self.res.at[c, self.half(self.core)]
        return self.send(part, part, self.p6s.at[c], self.p6r.at[c], self.mate)

    def each(self, make, c):
        return [make(c, k, d) for d in (1, 3, 2) for k in range(3)]

    def phase(self, i, c):
        core = self.core
        if i == 0:
            self.c0(c).start()
        elif i == 1:
            self.c0(c).wait_recv()
            mine = self.half(core)
            self.cb[c, mine, :] = self.cb[c, mine, :] + self.pbuf[c]
            for x in self.each(self.c1, c):
                x.start()
        elif i == 2:
            for k in range(3):
                for d in (1, 3, 2):
                    self.c1(c, k, d).wait_recv()
                self.total(c, k, self.r1, self.rows(k, self.coord[k]), self.coord[k], COLOR_ROWS[k] // N4, self.cb)
                for d in (1, 3, 2):
                    self.c2(c, k, d).start()
        elif i == 3:
            for k in range(3):
                for d in (1, 3, 2):
                    self.c2(c, k, d).wait_recv()
                b = (k + 1) % 3
                self.total(c, k, self.r2, self.rows(k, self.coord[k], self.coord[b]), self.coord[b], COLOR_ROWS[k] // N16, self.cb)
                for d in (1, 3, 2):
                    self.c3(c, k, d).start()
        elif i == N4:
            for k in range(3):
                for d in (1, 3, 2):
                    self.c3(c, k, d).wait_recv()
                b = (k + 2) % 3
                self.total(c, k, self.r3, self.rows(k, self.coord[k], self.coord[(k + 1) % 3]), self.coord[b], COLOR_ROWS[k] // N16, self.res)
                for d in (1, 3, 2):
                    self.c4(c, k, d).start()
        elif i == 5:
            for k in range(3):
                for d in (1, 3, 2):
                    self.c4(c, k, d).wait_recv()
                for d in (1, 3, 2):
                    self.c5(c, k, d).start()
        elif i == 6:
            for k in range(3):
                for d in (1, 3, 2):
                    self.c5(c, k, d).wait_recv()
            self.c6(c).start()
        elif i == 7:
            self.c6(c).wait_recv()

    def total(self, c, k, slots, rows, a, n, out):
        slots[c, k, a, 0:n, :] = self.cb[c, rows, :]
        out[c, rows, :] = (slots[c, k, 0, 0:n, :] + slots[c, k, 1, 0:n, :]) + (slots[c, k, 2, 0:n, :] + slots[c, k, 3, 0:n, :])

    def finish(self, c):
        self.c0(c).wait_send()
        for make in (self.c1, self.c2, self.c3, self.c4, self.c5):
            for x in self.each(make, c):
                x.wait_send()
        self.c6(c).wait_send()


def reducer_scratch():
    sem = pltpu.SemaphoreType.DMA
    bufs = [pltpu.VMEM((N4, 2048, N128), F32), pltpu.VMEM((N4, N1024, N128), F32), pltpu.VMEM((N4, 3, N4, 96, N128), F32),
            pltpu.VMEM((N4, 3, N4, 24, N128), F32), pltpu.VMEM((N4, 3, N4, 24, N128), F32)]
    sems = [sem((N4,)), sem((N4,))] + [sem((N4, 3, N4))] * 10 + [sem((N4,)), sem((N4,))]
    return bufs, sems


def write_out(res, outs, sem, t):
    copies = []
    cols = pl.ds(pl.multiple_of(N128 * t, N128), N128)
    for i in range(3):
        copies.append(pltpu.make_async_copy(res.at[t, pl.ds(N512 * i, N512)], outs[i].at[:, cols], sem.at[t, i]))
    for j in range(N4):
        copies.append(pltpu.make_async_copy(res.at[t, pl.ds(1536 + N128 * j, N128)], outs[3].at[cols, pl.ds(N128 * j, N128)], sem.at[t, 3 + j]))
    return copies


def attention_kernel(x_ref, wq_ref, wk_ref, wv_ref, wo_ref, dy_ref, y_hbm, dx_hbm, o0, o1, o2, o3,
                     xp, dyp, qm, kt, vt, dom, g2, g3, est, ms, mh, lh, oh, lseh, delh, dqh, dka, dva, attnb, grads,
                     st2, st3, colt, rowt, s2s, s2r, s3s, s3r, t2s, t2r, t3s, t3r, y_ref, dx_ref, cb, res, pbuf, r1, r2, r3, wsem, osem, *rsems):
    red = Reducer(cb, res, pbuf, r1, r2, r3, rsems)
    me = lax.axis_index("sp")
    member = me % N4
    base = me - member
    peers = [None, base + (member + 1 - 2 * (member % 2)), base + (member + 2 - N4 * (member // 2)), base + 3 - member]

    barrier = pltpu.get_barrier_semaphore()
    everyone = [peers[1], peers[3]] + [red.peer(ax, d) for ax in range(3) for d in (1, 2, 3)]
    for p in everyone:
        pl.semaphore_signal(barrier, inc=1, device_id={"sp": p}, device_id_type=MESH)

    ri = lax.broadcasted_iota(jnp.int32, (N256, N256), 0)
    ci = lax.broadcasted_iota(jnp.int32, (N256, N256), 1)

    def token_of(i):
        blk = i >> 5
        return ((i & 31) << 3) + ((blk & 1) << 2) + (blk & 2) + (blk >> 2)

    one = jnp.ones((), F32)
    zero = jnp.zeros((), F32)
    perm = jnp.where(token_of(ri) == ci, one, zero).astype(BF16)
    for s in range(2):
        rows = slice(N256 * s, N256 * s + N256)
        xp[rows, :] = dot(perm, x_ref[rows, :]).astype(BF16)
        dyp[rows, :] = dot(perm, dy_ref[rows, :]).astype(BF16)

    low = lanes_low(N512)
    keep = [jnp.where(low, one, zero).astype(BF16), jnp.where(low, zero, one).astype(BF16)]

    for half in range(2):
        cols = slice(N256 * half, N256 * half + N256)
        qq = dot(xp[...], wq_ref[:, cols]).astype(BF16) * jnp.asarray(HEAD_DIM ** -0.5, BF16)
        kk = dot(xp[...], wk_ref[:, cols]).astype(BF16)
        vv = dot(xp[...], wv_ref[:, cols]).astype(BF16)
        dd = dot(dyp[...], wo_ref[cols, :], NT).astype(BF16)
        for u in range(2):
            t = 2 * half + u
            lanes = slice(N128 * u, N128 * u + N128)
            kt[t] = kk[:, lanes]
            vt[t] = vv[:, lanes]
            for par in range(2):
                qm[par, t] = qq[:, lanes] * keep[par]
                dom[par, t] = dd[:, lanes] * keep[par]
            for g, n, off in ((g2, N64, N64 * (t & 1)), (g3, N32, N32 * (2 * (t & 1) + (t >> 1)))):
                for a, ref in ((0, kk), (1, vv)):
                    for s in range(2):
                        r = N256 * s + off
                        g[a, t, n * s:n * s + n, :] = ref[r:r + n, lanes] * keep[0][:n] + ref[r + N128:r + N128 + n, lanes] * keep[1][:n]
                for a, ref in ((2, qq), (3, dd)):
                    for s in range(2):
                        r = N256 * s + off
                        g[a, t, n * s:n * s + n, :] = ref[r:r + n, lanes] * keep[0][:n] + ref[r + N128:r + N128 + n, lanes] * keep[1][:n]

    pl.semaphore_wait(barrier, len(everyone))
    copies2 = []
    copies3 = []
    for a in range(N4):
        c = pltpu.make_async_remote_copy(src_ref=g2.at[a, :, pl.ds(0, N128), :], dst_ref=g2.at[a, :, pl.ds(N128, N128), :],
                                         send_sem=s2s.at[a], recv_sem=s2r.at[a], device_id={"sp": peers[1]}, device_id_type=MESH)
        c.start()
        copies2.append(c)
    for a in range(N4):
        row = []
        for d in (2, 3, 1):
            c = pltpu.make_async_remote_copy(src_ref=g3.at[a, :, pl.ds(0, N64), :], dst_ref=g3.at[a, :, pl.ds(N64 * d, N64), :],
                                             send_sem=s3s.at[a, d], recv_sem=s3r.at[a, d], device_id={"sp": peers[d]}, device_id_type=MESH)
            c.start()
            row.append(c)
        copies3.append(row)

    def forward(q, k, v):
        s = dot(q, k, NT)
        m = jnp.max(s, axis=1, keepdims=True)
        e = jnp.exp(s - m)
        l = jnp.sum(e, axis=1, keepdims=True)
        o = dot(e.astype(BF16), v)
        n = q.shape[0]
        return jnp.broadcast_to(m, (n, N128)), jnp.broadcast_to(l, (n, N128)), o, e

    def merge(t, par, start, n, m, l, o):
        m0 = two(mh, (t, par), start, n)
        l0 = two(lh, (t, par), start, n)
        o0 = two(oh, (t, par), start, n)
        mn = jnp.maximum(m0, m)
        a = jnp.exp(m0 - mn)
        b = jnp.exp(m - mn)
        put_two(mh, (t, par), start, n, mn)
        put_two(lh, (t, par), start, n, l0 * a + l * b)
        put_two(oh, (t, par), start, n, o0 * a + o * b)

    def off2(t, par):
        return pl.multiple_of(N128 * par + N64 * (t % 2), N64)

    def off3(t, par):
        return pl.multiple_of(N128 * par + N64 * (t % 2) + N32 * (t // 2), N32)

    def fwd_local(t, carry):
        for par in range(2):
            for s in range(2):
                rows = slice(N256 * s, N256 * s + N256)
                m, l, o, e = forward(qm[par, t, rows, :], kt[t, rows, :], vt[t, rows, :])
                mh[t, par, rows, :] = m
                lh[t, par, rows, :] = l
                oh[t, par, rows, :] = o
                ms[t, par, rows, :] = m
                est[t, par, rows, :] = e
            m, l, o, e = forward(two(qm, (par, t), N128 * par, N128), two(kt, (t,), N128 * par, N128), two(vt, (t,), N128 * par, N128))
            ms[t, par, N512:N768, :] = m
            est[t, par, N512:N768, :] = e
            merge(t, par, N128 * par, N128, m, l, o)
        return carry

    lax.fori_loop(0, N4, fwd_local, 0)

    for a in range(2):
        copies2[a].wait_recv()
        for c in copies3[a]:
            c.wait_recv()

    low256 = lanes_low(N256)
    colt[...] = jnp.zeros_like(colt)

    def fwd_group(t, carry):
        atts = []
        for par in range(2):
            o2 = off2(t, par)
            m, l, o, e = forward(two(qm, (par, t), o2, N64), g2[0, t], g2[1, t])
            ms[t, par, N768:N896, :] = m
            est[t, par, N768:N896, :] = e
            merge(t, par, o2, N64, m, l, o)
            o3 = off3(t, par)
            m, l, o, e = forward(two(qm, (par, t), o3, N32), g3[0, t], g3[1, t])
            ms[t, par, N896:960, :] = m
            est[t, par, N896:960, :] = e
            merge(t, par, o3, N32, m, l, o)
            lt = lh[t, par]
            att = oh[t, par] / lt
            lse = mh[t, par] + jnp.log(lt)
            delta = jnp.broadcast_to(jnp.sum(dom[par, t].astype(F32) * att, axis=1, keepdims=True), (N512, N128))
            lseh[t, par] = lse
            delh[t, par] = delta
            atts.append(att)
            h = 2 * t + par
            lane = lax.broadcasted_iota(jnp.int32, (N512, N128), 1)
            colt[0:N512, :] = jnp.where(lane == h, lse, jnp.where(lane == h + N8, delta, colt[0:N512, :]))
            l2 = two(lseh, (t, par), o2, N64)
            d2 = two(delh, (t, par), o2, N64)
            colt[N512:N640, :] = jnp.where(lane[:N128] == h, l2, jnp.where(lane[:N128] == h + N8, d2, colt[N512:N640, :]))
            l3 = two(lseh, (t, par), o3, N32)
            d3 = two(delh, (t, par), o3, N32)
            l3 = jnp.concatenate([l3, l3], axis=0)
            d3 = jnp.concatenate([d3, d3], axis=0)
            colt[N640:N768, :] = jnp.where(lane[:N128] == h, l3, jnp.where(lane[:N128] == h + N8, d3, colt[N640:N768, :]))
        attnb[:, pl.ds(pl.multiple_of(N128 * t, N128), N128)] = jnp.where(low, atts[0], atts[1]).astype(BF16)
        return carry

    lax.fori_loop(0, N4, fwd_group, 0)

    st2[0] = jnp.transpose(colt[N512:N640, :])[:N16]
    st3[0] = jnp.transpose(colt[N640:N768, :])[:N16]
    for j in range(N4):
        r = jnp.transpose(colt[N128 * j:N128 * j + N128, :])
        rowt[:, N128 * j:N128 * j + N128] = r[:N16]
    stat2 = pltpu.make_async_remote_copy(src_ref=st2.at[0], dst_ref=st2.at[1], send_sem=t2s, recv_sem=t2r,
                                         device_id={"sp": peers[1]}, device_id_type=MESH)
    stat2.start()
    stats3 = []
    for d in (2, 3, 1):
        c = pltpu.make_async_remote_copy(src_ref=st3.at[0], dst_ref=st3.at[d], send_sem=t3s.at[d], recv_sem=t3r.at[d],
                                         device_id={"sp": peers[d]}, device_id_type=MESH)
        c.start()
        stats3.append(c)

    def grad_q(d_rows, k, v, e, delta):
        dp = dot(d_rows, v, NT)
        ds = (e * (dp - wide(delta))).astype(BF16)
        return dot(ds, k)

    def grad_kv(q, d_rows, k, v, lse_row, delta_row):
        st = dot(k, q, NT)
        pt = jnp.exp(st - lse_row)
        dpt = dot(v, d_rows, NT)
        dst = (pt * (dpt - delta_row)).astype(BF16)
        return dot(dst, q), dot(pt.astype(BF16), d_rows)

    def row_of(ref, lead, i):
        return ref[lead + (pl.ds(i, 1), slice(None))]

    def bwd_local(t, par):
        if True:
            h = 2 * t + par
            lse_row = row_of(rowt, (), h)
            del_row = row_of(rowt, (), h + N8)
            for s in range(2):
                rows = slice(N256 * s, N256 * s + N256)
                dr = dom[par, t, rows, :]
                kr = kt[t, rows, :]
                vr = vt[t, rows, :]
                lse = lseh[t, par, rows, :]
                dqj = grad_q(dr, kr, vr, est[t, par, rows, :], delh[t, par, rows, :])
                dqh[par, rows, :] = dqj * jnp.exp(ms[t, par, rows, :] - lse)
                gk, gv = grad_kv(qm[par, t, rows, :], dr, kr, vr, lse_row[:, rows], del_row[:, rows])
                if par == 0:
                    dka[t, rows, :] = gk
                    dva[t, rows, :] = gv
                else:
                    dka[t, rows, :] += gk
                    dva[t, rows, :] += gv
            a = N128 * par
            dr = two(dom, (par, t), a, N128)
            kr = two(kt, (t,), a, N128)
            vr = two(vt, (t,), a, N128)
            f = jnp.exp(ms[t, par, N512:N768, :] - two(lseh, (t, par), a, N128))
            dqj = f * grad_q(dr, kr, vr, est[t, par, N512:N768, :], two(delh, (t, par), a, N128))
            put_two(dqh, (par,), a, N128, two(dqh, (par,), a, N128) + dqj)
            lr = jnp.concatenate([lse_row[:, a:a + N128], lse_row[:, N256 + a:N256 + a + N128]], axis=1)
            dlr = jnp.concatenate([del_row[:, a:a + N128], del_row[:, N256 + a:N256 + a + N128]], axis=1)
            gk, gv = grad_kv(two(qm, (par, t), a, N128), dr, kr, vr, lr, dlr)
            put_two(dka, (t,), a, N128, two(dka, (t,), a, N128) + gk)
            put_two(dva, (t,), a, N128, two(dva, (t,), a, N128) + gv)
            for lo, n, off, g in ((N768, N64, off2(t, par), g2), (N896, N32, off3(t, par), g3)):
                f = jnp.exp(ms[t, par, lo:lo + 2 * n, :] - two(lseh, (t, par), off, n))
                dqj = f * grad_q(two(dom, (par, t), off, n), g[0, t], g[1, t], est[t, par, lo:lo + 2 * n, :], two(delh, (t, par), off, n))
                put_two(dqh, (par,), off, n, two(dqh, (par,), off, n) + dqj)

    keep256 = [keep[0][:N256], keep[1][:N256]]

    def bwd_group(t, par):
        if True:
            h = 2 * t + par
            lr = jnp.concatenate([row_of(st2, (0,), h), row_of(st2, (1,), h)], axis=1)
            dlr = jnp.concatenate([row_of(st2, (0,), h + N8), row_of(st2, (1,), h + N8)], axis=1)
            off = off2(t, par)
            gk, gv = grad_kv(g2[2, t] * keep256[par], g2[3, t] * keep256[par], two(kt, (t,), off, N64), two(vt, (t,), off, N64), lr, dlr)
            put_two(dka, (t,), off, N64, two(dka, (t,), off, N64) + gk)
            put_two(dva, (t,), off, N64, two(dva, (t,), off, N64) + gv)
            lo = lax.broadcasted_iota(jnp.int32, (1, N128), 1) < N64
            lr = jnp.concatenate([jnp.where(lo, row_of(st3, (0,), h), row_of(st3, (1,), h)), jnp.where(lo, row_of(st3, (2,), h), row_of(st3, (3,), h))], axis=1)
            dlr = jnp.concatenate([jnp.where(lo, row_of(st3, (0,), h + N8), row_of(st3, (1,), h + N8)), jnp.where(lo, row_of(st3, (2,), h + N8), row_of(st3, (3,), h + N8))], axis=1)
            off = off3(t, par)
            gk, gv = grad_kv(g3[2, t] * keep256[par], g3[3, t] * keep256[par], two(kt, (t,), off, N32), two(vt, (t,), off, N32), lr, dlr)
            put_two(dka, (t,), off, N32, two(dka, (t,), off, N32) + gk)
            put_two(dva, (t,), off, N32, two(dva, (t,), off, N32) + gv)

    def chunk(t):
        cols = slice(N128 * t, N128 * t + N128)
        dq = jnp.where(low, dqh[0], dqh[1]) * (HEAD_DIM ** -0.5)
        for i, g in enumerate((dq, dka[t], dva[t])):
            gb = g.astype(BF16)
            grads[i, :, cols] = gb
            cb[t, N512 * i:N512 * i + N512, :] = dot(xp[...], gb, TN)
        g = dot(attnb[:, cols], dyp[...], TN)
        for j in range(N4):
            cb[t, 1536 + N128 * j:1664 + N128 * j, :] = g[:, N128 * j:N128 * j + N128]

    def step(t, lag):
        for c in range(t + 1):
            i = lag - 2 * c
            if 0 <= i <= 7:
                red.phase(i, c)
                if i == 7:
                    for x in write_out(res, (o0, o1, o2, o3), wsem, c):
                        x.start()

    for t in range(N4):
        bwd_local(t, 0)
        bwd_local(t, 1)
        step(t - 1, 2 * t - 1)
        if t == 0:
            stat2.wait_recv()
            for c in stats3:
                c.wait_recv()
            for a in (2, 3):
                copies2[a].wait_recv()
                for c in copies3[a]:
                    c.wait_recv()
        bwd_group(t, 0)
        bwd_group(t, 1)
        chunk(t)
        step(t, 2 * t)

    def y_part(s):
        rows = slice(N256 * s, N256 * s + N256)
        yb = dot(attnb[rows, :], wo_ref[...]).astype(BF16)
        y_ref[rows, :] = dot(perm, yb, TN).astype(BF16)

    def dx_part(s):
        rows = slice(N256 * s, N256 * s + N256)
        dxb = (dot(grads[0, rows, :], wq_ref[...], NT) + dot(grads[1, rows, :], wk_ref[...], NT) + dot(grads[2, rows, :], wv_ref[...], NT)).astype(BF16)
        dx_ref[rows, :] = dot(perm, dxb, TN).astype(BF16)

    y_out = pltpu.make_async_copy(y_ref, y_hbm, osem.at[0])
    dx_out = pltpu.make_async_copy(dx_ref, dx_hbm, osem.at[1])
    work = [functools.partial(dx_part, 0), functools.partial(dx_part, 1), functools.partial(y_part, 0), functools.partial(y_part, 1)]
    for lag in range(7, 14):
        if work:
            work.pop(0)()
        elif lag == 11:
            y_out.start()
            dx_out.start()
        step(3, lag)

    for c in copies2:
        c.wait_send()
    for row in copies3:
        for c in row:
            c.wait_send()
    stat2.wait_send()
    for c in stats3:
        c.wait_send()
    for c in range(N4):
        red.finish(c)
        for x in write_out(res, (o0, o1, o2, o3), wsem, c):
            x.wait()
    y_out.wait()
    dx_out.wait()


def attention(x_loc, w_q, w_k, w_v, w_o, dy_loc):
    vmem = pl.BlockSpec(memory_space=pltpu.VMEM)
    sem = pltpu.SemaphoreType.DMA
    bufs, sems = reducer_scratch()
    return pl.pallas_call(
        attention_kernel,
        out_shape=[jax.ShapeDtypeStruct((N512, N512), BF16)] * 2 + [jax.ShapeDtypeStruct((N512, N512), F32)] * N4,
        in_specs=[vmem] * 6,
        out_specs=[pl.BlockSpec(memory_space=pl.ANY)] * 6,
        scratch_shapes=[
            pltpu.VMEM((N512, N512), BF16), pltpu.VMEM((N512, N512), BF16),
            pltpu.VMEM((2, N4, N512, N128), BF16), pltpu.VMEM((N4, N512, N128), BF16), pltpu.VMEM((N4, N512, N128), BF16), pltpu.VMEM((2, N4, N512, N128), BF16),
            pltpu.VMEM((N4, N4, N256, N128), BF16), pltpu.VMEM((N4, N4, N256, N128), BF16),
            pltpu.VMEM((N4, 2, 960, N256), F32), pltpu.VMEM((N4, 2, 960, N128), F32),
            pltpu.VMEM((N4, 2, N512, N128), F32), pltpu.VMEM((N4, 2, N512, N128), F32), pltpu.VMEM((N4, 2, N512, N128), F32),
            pltpu.VMEM((N4, 2, N512, N128), F32), pltpu.VMEM((N4, 2, N512, N128), F32),
            pltpu.VMEM((2, N512, N128), F32), pltpu.VMEM((N4, N512, N128), F32), pltpu.VMEM((N4, N512, N128), F32),
            pltpu.VMEM((N512, N512), BF16), pltpu.VMEM((3, N512, N512), BF16),
            pltpu.VMEM((2, N16, N128), F32), pltpu.VMEM((N4, N16, N128), F32), pltpu.VMEM((N768, N128), F32), pltpu.VMEM((N16, N512), F32),
            sem((N4,)), sem((N4,)), sem((N4, N4)), sem((N4, N4)), sem, sem, sem((N4,)), sem((N4,)),
            pltpu.VMEM((N512, N512), BF16), pltpu.VMEM((N512, N512), BF16), pltpu.VMEM((N4, 2048, N128), F32),
        ] + bufs + [sem((N4, 7)), sem((2,))] + sems,
        compiler_params=pltpu.CompilerParams(collective_id=0, has_side_effects=True, vmem_limit_bytes=60 * 2 ** 20),
        name="attention_step",
    )(x_loc, w_q, w_k, w_v, w_o, dy_loc)


def solution(mesh):
    def device_step(x_loc, w_q, w_k, w_v, w_o, dy_loc):
        return tuple(attention(x_loc, w_q, w_k, w_v, w_o, dy_loc))

    row_spec = P(("dp", "sp"), None)
    full_spec = P(None, None)
    grad_spec = P("dp", None)
    return jax.shard_map(device_step, mesh=mesh, in_specs=(row_spec, full_spec, full_spec, full_spec, full_spec, row_spec),
                         out_specs=(row_spec, row_spec, grad_spec, grad_spec, grad_spec, grad_spec), check_vma=False)
```

time: 215 us -> 94.3 us (0.44)
  waiting for transfers between devices: 157 us -> 0 us
  Pallas kernels: 38.3 us -> 84.8 us
  between operations: 14.1 us -> 0.66 us
  local copies, waits for them, and re-layouts: 5.84 us -> 8.56 us
    psum x1 -> x0, waiting for transfers between devices: 157 us -> none  [device_step(): dws = lax.psum(dws, 'sp')]
    pallas_call x1, Pallas kernels: 38.3 us -> 84.8 us  [attention(): pl.pallas_call(attention_kernel, out_shape=[jax.ShapeDtypeStruct((N512, N...]
    unnamed x6 -> x16, local copies, waits for them, and re-layouts: 1.59 us -> 8.56 us
    squeeze x1 -> x0, local copies, waits for them, and re-layouts: 4.25 us -> none  [device_step(): return (y_loc, dx_loc, dws[0], dws[1], dws[2], dws[3])]
  transfers between devices with their start and end apart: 1 -> 0, of which waited for: 1 -> 0; matrix products, arithmetic and copies ran while one was open for 0% -> 0% of each run, Pallas kernels for 0% -> 0%
where the time goes in v2:
time: 94.3 us; the launch traced here: 94 us
  Pallas kernels  84.8 us (90%)
  local copies, waits for them, and re-layouts  8.56 us (9%)
    pallas_call x1, Pallas kernels, attention(): pl.pallas_call(attention_kernel, out_shape=[jax.ShapeDtypeStruct((N512, N...  84.8 us
    unnamed x16, local copies, waits for them, and re-layouts  8.56 us

profile of v2, /device:TPU:1, one launch (start us, length us, event | category | flops | bytes accessed | tf_op | source)
XLA Modules:
  0.0 94.0 jit_solution(16830175473007183459)
XLA Ops:
  0.6 84.8 %attention_step.1 = (bf16[512,512]{1,0:T(8,128)(2,1)}, bf16[512,512]{1,0:T(8,128)(2,1)}, f32[512,512]{1,0:T(8,128)}, f32[512,512]{1,0:T(8,128)}, f32[512,512]{1,0:T(8,128)}, /*index=5*/f32[512,512]{1,0:T(8,128)}) custom-call(bf16[512,512]{1,0:T(8,128)(2,1)} %x_ref.1, bf16[512,512]{1,0:T(8,128)(2,1)} %wq_ref.1, bf16[512,512]{1,0:T(8,128)(2,1)} %wk_ref.1, ...), custom_call_target="tpu_custom_call" | custom-call | tf_op jit(solution)/shard_map/attention_step/pallas_call | solution.py:523
  85.5 0.0 copy-start.4
  85.5 0.0 copy-start.3
  85.5 2.0 %copy.18 = bf16[512,512]{1,0:T(8,128)(2,1)} copy(bf16[512,512]{1,0:T(8,128)(2,1)} %get-tuple-element.12) | data formatting | bytes 1048576
  87.5 0.0 copy-done.4
  87.5 0.8 copy.19
  88.3 0.0 copy-done.3
  88.3 0.0 copy-start.2
  88.3 1.0 %copy.20 = f32[512,512]{1,0:T(8,128)} copy(f32[512,512]{1,0:T(8,128)S(1)} %copy-done.3) | data formatting | bytes 2097152
  89.2 0.6 copy-done.2
  89.9 0.0 copy-start.1
  89.9 1.0 %copy.21 = f32[512,512]{1,0:T(8,128)} copy(f32[512,512]{1,0:T(8,128)S(1)} %copy-done.2) | data formatting | bytes 2097152
  90.8 0.6 copy-done.1
  91.5 0.0 copy-start
  91.5 1.0 %copy.22 = f32[512,512]{1,0:T(8,128)} copy(f32[512,512]{1,0:T(8,128)S(1)} %copy-done.1) | data formatting | bytes 2097152
  92.4 0.6 copy-done
  93.1 1.0 %copy.23 = f32[512,512]{1,0:T(8,128)} copy(f32[512,512]{1,0:T(8,128)S(1)} %copy-done) | data formatting | bytes 2097152
Async XLA Ops:
  85.5 2.0 %copy-start.4 = (bf16[512,512]{1,0:T(8,128)(2,1)S(1)}, bf16[512,512]{1,0:T(8,128)(2,1)}, u32[]{:S(2)}) copy-start(bf16[512,512]{1,0:T(8,128)(2,1)} %get-tuple-element.13) | copy-start | bytes 1572868
  85.5 2.8 %copy-start.3 = (f32[512,512]{1,0:T(8,128)S(1)}, f32[512,512]{1,0:T(8,128)}, u32[]{:S(2)}) copy-start(f32[512,512]{1,0:T(8,128)} %get-tuple-element.14) | copy-start | bytes 3145732
  88.3 1.6 %copy-start.2 = (f32[512,512]{1,0:T(8,128)S(1)}, f32[512,512]{1,0:T(8,128)}, u32[]{:S(2)}) copy-start(f32[512,512]{1,0:T(8,128)} %get-tuple-element.15) | copy-start | bytes 3145732
  89.9 1.6 %copy-start.1 = (f32[512,512]{1,0:T(8,128)S(1)}, f32[512,512]{1,0:T(8,128)}, u32[]{:S(2)}) copy-start(f32[512,512]{1,0:T(8,128)} %get-tuple-element.16) | copy-start | bytes 3145732
  91.5 1.6 %copy-start = (f32[512,512]{1,0:T(8,128)S(1)}, f32[512,512]{1,0:T(8,128)}, u32[]{:S(2)}) copy-start(f32[512,512]{1,0:T(8,128)} %get-tuple-element.17) | copy-start | bytes 3145732

commit v3 on v2

v3 whole, which is shorter than its diff:
```python
import functools

import jax
import jax.numpy as jnp
from jax import lax
from jax.experimental import pallas as pl
from jax.experimental.pallas import tpu as pltpu
from jax.sharding import PartitionSpec as P

HEAD_DIM = 64
N4 = 4
N8 = 8
N16 = 16
N32 = 32
N64 = 64
N128 = 128
N256 = 256
N512 = 512
N640 = 640
N768 = 768
N1024 = 1024
F32 = jnp.float32
BF16 = jnp.bfloat16
MESH = pl.DeviceIdType.MESH
NN = (((1,), (0,)), ((), ()))
NT = (((1,), (1,)), ((), ()))
TN = (((0,), (0,)), ((), ()))


def dot(a, b, dims=NN):
    return lax.dot_general(a, b, dims, preferred_element_type=F32)


def two(ref, lead, start, n):
    return jnp.concatenate([ref[lead + (pl.ds(start, n), slice(None))], ref[lead + (pl.ds(N256 + start, n), slice(None))]], axis=0)


def put_two(ref, lead, start, n, val):
    ref[lead + (pl.ds(start, n), slice(None))] = val[:n]
    ref[lead + (pl.ds(N256 + start, n), slice(None))] = val[n:]


def wide(stat):
    return jnp.concatenate([stat, stat], axis=1)


def add_two(ref, lead, start, n, val):
    put_two(ref, lead, start, n, two(ref, lead, start, n) + val)


def lanes_low(rows):
    return lax.broadcasted_iota(jnp.int32, (rows, N128), 1) < N64


COLOR_ROWS = (384, 384, N256)
COLOR_BASE = (0, 384, N768)
STRIDES = (2, N8, N32)


class Reducer:
    def __init__(self, cb, res, pbuf, r1, r2, r3, sems):
        self.cb, self.res, self.pbuf, self.r1, self.r2, self.r3 = cb, res, pbuf, r1, r2, r3
        (self.p0s, self.p0r, self.p1s, self.p1r, self.p2s, self.p2r, self.p3s, self.p3r,
         self.p4s, self.p4r, self.p5s, self.p5r, self.p6s, self.p6r) = sems
        self.me = lax.axis_index("sp")
        self.core = self.me % 2
        self.coord = [(self.me // s) % N4 for s in STRIDES]
        self.mate = self.me + 1 - 2 * self.core

    def peer(self, axis, d):
        return self.me + STRIDES[axis] * ((self.coord[axis] + d) % N4 - self.coord[axis])

    def send(self, src, dst, ss, rs, dev):
        return pltpu.make_async_remote_copy(src_ref=src, dst_ref=dst, send_sem=ss, recv_sem=rs, device_id={"sp": dev}, device_id_type=MESH)

    def half(self, core):
        return pl.ds(pl.multiple_of(N1024 * core, N1024), N1024)

    def rows(self, k, q, p=None):
        n = COLOR_ROWS[k]
        start = N1024 * self.core + COLOR_BASE[k] + (n // N4) * q
        if p is None:
            return pl.ds(pl.multiple_of(start, N8), n // N4)
        return pl.ds(pl.multiple_of(start + (n // N16) * p, N8), n // N16)

    def c0(self, c):
        return self.send(self.cb.at[c, self.half(1 - self.core)], self.pbuf.at[c], self.p0s.at[c], self.p0r.at[c], self.mate)

    def c1(self, c, k, d):
        n = COLOR_ROWS[k] // N4
        a = self.coord[k]
        return self.send(self.cb.at[c, self.rows(k, (a + d) % N4)], self.r1.at[c, k, a, pl.ds(0, n)], self.p1s.at[c, k, d], self.p1r.at[c, k, d], self.peer(k, d))

    def c2(self, c, k, d):
        n = COLOR_ROWS[k] // N16
        b = (k + 1) % 3
        a = self.coord[b]
        src = self.cb.at[c, self.rows(k, self.coord[k], (a + d) % N4)]
        return self.send(src, self.r2.at[c, k, a, pl.ds(0, n)], self.p2s.at[c, k, d], self.p2r.at[c, k, d], self.peer(b, d))

    def c3(self, c, k, d):
        n = COLOR_ROWS[k] // N16
        b = (k + 2) % 3
        a = self.coord[b]
        src = self.cb.at[c, self.rows(k, self.coord[k], self.coord[(k + 1) % 3])]
        return self.send(src, self.r3.at[c, k, a, pl.ds(0, n)], self.p3s.at[c, k, d], self.p3r.at[c, k, d], self.peer(b, d))

    def c4(self, c, k, d):
        b = (k + 1) % 3
        part = self.res.at[c, self.rows(k, self.coord[k], self.coord[b])]
        return self.send(part, part, self.p4s.at[c, k, d], self.p4r.at[c, k, d], self.peer(b, d))

    def c5(self, c, k, d):
        part = self.res.at[c, self.rows(k, self.coord[k])]
        return self.send(part, part, self.p5s.at[c, k, d], self.p5r.at[c, k, d], self.peer(k, d))

    def c6(self, c):
        part = self.res.at[c, self.half(self.core)]
        return self.send(part, part, self.p6s.at[c], self.p6r.at[c], self.mate)

    def each(self, make, c):
        return [make(c, k, d) for d in (1, 3, 2) for k in range(3)]

    def phase(self, i, c):
        core = self.core
        if i == 0:
            self.c0(c).start()
        elif i == 1:
            self.c0(c).wait_recv()
            mine = self.half(core)
            self.cb[c, mine, :] = self.cb[c, mine, :] + self.pbuf[c]
            for x in self.each(self.c1, c):
                x.start()
        elif i == 2:
            for k in range(3):
                for d in (1, 3, 2):
                    self.c1(c, k, d).wait_recv()
                self.total(c, k, self.r1, self.rows(k, self.coord[k]), self.coord[k], COLOR_ROWS[k] // N4, self.cb)
                for d in (1, 3, 2):
                    self.c2(c, k, d).start()
        elif i == 3:
            for k in range(3):
                for d in (1, 3, 2):
                    self.c2(c, k, d).wait_recv()
                b = (k + 1) % 3
                self.total(c, k, self.r2, self.rows(k, self.coord[k], self.coord[b]), self.coord[b], COLOR_ROWS[k] // N16, self.cb)
                for d in (1, 3, 2):
                    self.c3(c, k, d).start()
        elif i == N4:
            for k in range(3):
                for d in (1, 3, 2):
                    self.c3(c, k, d).wait_recv()
                b = (k + 2) % 3
                self.total(c, k, self.r3, self.rows(k, self.coord[k], self.coord[(k + 1) % 3]), self.coord[b], COLOR_ROWS[k] // N16, self.res)
                for d in (1, 3, 2):
                    self.c4(c, k, d).start()
        elif i == 5:
            for k in range(3):
                for d in (1, 3, 2):
                    self.c4(c, k, d).wait_recv()
                for d in (1, 3, 2):
                    self.c5(c, k, d).start()
        elif i == 6:
            for k in range(3):
                for d in (1, 3, 2):
                    self.c5(c, k, d).wait_recv()
            self.c6(c).start()
        elif i == 7:
            self.c6(c).wait_recv()

    def total(self, c, k, slots, rows, a, n, out):
        slots[c, k, a, 0:n, :] = self.cb[c, rows, :]
        out[c, rows, :] = (slots[c, k, 0, 0:n, :] + slots[c, k, 1, 0:n, :]) + (slots[c, k, 2, 0:n, :] + slots[c, k, 3, 0:n, :])

    def finish(self, c):
        self.c0(c).wait_send()
        for make in (self.c1, self.c2, self.c3, self.c4, self.c5):
            for x in self.each(make, c):
                x.wait_send()
        self.c6(c).wait_send()


def reducer_scratch():
    sem = pltpu.SemaphoreType.DMA
    bufs = [pltpu.VMEM((N4, 2048, N128), F32), pltpu.VMEM((N4, N1024, N128), F32), pltpu.VMEM((N4, 3, N4, 96, N128), F32),
            pltpu.VMEM((N4, 3, N4, 24, N128), F32), pltpu.VMEM((N4, 3, N4, 24, N128), F32)]
    sems = [sem((N4,)), sem((N4,))] + [sem((N4, 3, N4))] * 10 + [sem((N4,)), sem((N4,))]
    return bufs, sems


def write_out(res, outs, sem, t):
    copies = []
    cols = pl.ds(pl.multiple_of(N128 * t, N128), N128)
    for i in range(3):
        copies.append(pltpu.make_async_copy(res.at[t, pl.ds(N512 * i, N512)], outs[i].at[:, cols], sem.at[t, i]))
    for j in range(N4):
        copies.append(pltpu.make_async_copy(res.at[t, pl.ds(1536 + N128 * j, N128)], outs[3].at[cols, pl.ds(N128 * j, N128)], sem.at[t, 3 + j]))
    return copies


def attention_kernel(x_ref, wq_ref, wk_ref, wv_ref, wo_ref, dy_ref, y_hbm, dx_hbm, o0, o1, o2, o3,
                     xp, dyp, qm, kt, vt, dom, g2, g3, keep, mh, lh, oh, lseh, delh, dqh, dka, dva, attnb, grads,
                     st2, st3, colt, rowt, s2s, s2r, s3s, s3r, t2s, t2r, t3s, t3r, y_buf, dx_buf, cb, res, pbuf, r1, r2, r3, wsem, osem, *rsems):
    red = Reducer(cb, res, pbuf, r1, r2, r3, rsems)
    me = red.me
    member = me % N4
    base = me - member
    peers = [None, red.mate, base + (member + 2 - N4 * (member // 2)), base + 3 - member]
    everyone = [peers[1], peers[3]] + [red.peer(ax, d) for ax in range(3) for d in (1, 2, 3)]

    barrier = pltpu.get_barrier_semaphore()
    for p in everyone:
        pl.semaphore_signal(barrier, inc=1, device_id={"sp": p}, device_id_type=MESH)

    ri = lax.broadcasted_iota(jnp.int32, (N256, N256), 0)
    ci = lax.broadcasted_iota(jnp.int32, (N256, N256), 1)
    blk = ri >> 5
    token = ((ri & 31) << 3) + ((blk & 1) << 2) + (blk & 2) + (blk >> 2)
    one = jnp.ones((), F32)
    zero = jnp.zeros((), F32)
    perm = jnp.where(token == ci, one, zero).astype(BF16)
    low = lanes_low(N512)
    keep[0] = jnp.where(low, one, zero).astype(BF16)
    keep[1] = jnp.where(low, zero, one).astype(BF16)

    def off2(t, par):
        return pl.multiple_of(N128 * par + N64 * (t % 2), N64)

    def off3(t, par):
        return pl.multiple_of(N128 * par + N64 * (t % 2) + N32 * (t // 2), N32)

    def lanes_of(i, n):
        return pl.ds(pl.multiple_of(i * n, n), n)

    def rows_of(s):
        return pl.ds(pl.multiple_of(N256 * s, N256), N256)

    for s in range(2):
        rows = slice(N256 * s, N256 * s + N256)
        xp[rows, :] = dot(perm, x_ref[rows, :]).astype(BF16)

    def project_kv(half, carry):
        cols = lanes_of(half, N256)
        for w, out in ((wk_ref, kt), (wv_ref, vt)):
            val = dot(xp[...], w[:, cols]).astype(BF16)
            out[2 * half] = val[:, :N128]
            out[2 * half + 1] = val[:, N128:]
        return carry

    def pack(a, ev, od, t):
        for g, n, off in ((g2, N64, N64 * (t % 2)), (g3, N32, N64 * (t % 2) + N32 * (t // 2))):
            for s in range(2):
                r = pl.multiple_of(N256 * s + off, N32)
                g[a, t, n * s:n * s + n, :] = ev(pl.ds(r, n)) * keep[0, :n, :] + od(pl.ds(r + N128, n)) * keep[1, :n, :]

    def pack_kv(t, carry):
        for a, ref in enumerate((kt, vt)):
            pack(a, lambda r: ref[t, r, :], lambda r: ref[t, r, :], t)
        return carry

    lax.fori_loop(0, 2, project_kv, 0)
    lax.fori_loop(0, N4, pack_kv, 0)

    def to2(a):
        return red.send(g2.at[a, :, pl.ds(0, N128), :], g2.at[a, :, pl.ds(N128, N128), :], s2s.at[a], s2r.at[a], peers[1])

    def to3(a, d):
        return red.send(g3.at[a, :, pl.ds(0, N64), :], g3.at[a, :, pl.ds(N64 * d, N64), :], s3s.at[a, d], s3r.at[a, d], peers[d])

    def send_group(arrays):
        for a in arrays:
            for d in (2, 3, 1):
                to3(a, d).start()
            to2(a).start()

    pl.semaphore_wait(barrier, len(everyone))
    send_group((0, 1))

    for s in range(2):
        rows = slice(N256 * s, N256 * s + N256)
        dyp[rows, :] = dot(perm, dy_ref[rows, :]).astype(BF16)

    def project_qo(half, carry):
        cols = lanes_of(half, N256)
        q = dot(xp[...], wq_ref[:, cols]).astype(BF16) * jnp.asarray(HEAD_DIM ** -0.5, BF16)
        d = dot(dyp[...], wo_ref[cols, :], NT).astype(BF16)
        for u in range(2):
            for par in range(2):
                qm[par, 2 * half + u] = q[:, N128 * u:N128 * u + N128] * keep[par]
                dom[par, 2 * half + u] = d[:, N128 * u:N128 * u + N128] * keep[par]
        return carry

    def pack_qo(t, carry):
        for a, ref in ((2, qm), (3, dom)):
            pack(a, lambda r: ref[0, t, r, :], lambda r: ref[1, t, r, :], t)
        return carry

    lax.fori_loop(0, 2, project_qo, 0)
    lax.fori_loop(0, N4, pack_qo, 0)
    send_group((2, 3))

    def forward(q, k, v):
        s = dot(q, k, NT)
        m = jnp.max(s, axis=1, keepdims=True)
        e = jnp.exp(s - m)
        l = jnp.sum(e, axis=1, keepdims=True)
        o = dot(e.astype(BF16), v)
        n = q.shape[0]
        return jnp.broadcast_to(m, (n, N128)), jnp.broadcast_to(l, (n, N128)), o

    def merge(h, start, n, m, l, o):
        m0 = two(mh, (h,), start, n)
        l0 = two(lh, (h,), start, n)
        o0 = two(oh, (h,), start, n)
        mn = jnp.maximum(m0, m)
        a = jnp.exp(m0 - mn)
        b = jnp.exp(m - mn)
        put_two(mh, (h,), start, n, mn)
        put_two(lh, (h,), start, n, l0 * a + l * b)
        put_two(oh, (h,), start, n, o0 * a + o * b)

    def fwd_local(h, carry):
        t, par = h // 2, h % 2
        for s in range(2):
            rows = slice(N256 * s, N256 * s + N256)
            m, l, o = forward(qm[par, t, rows, :], kt[t, rows, :], vt[t, rows, :])
            mh[h, rows, :] = m
            lh[h, rows, :] = l
            oh[h, rows, :] = o
        a = pl.multiple_of(N128 * par, N128)
        merge(h, a, N128, *forward(two(qm, (par, t), a, N128), two(kt, (t,), a, N128), two(vt, (t,), a, N128)))
        return carry

    lax.fori_loop(0, N8, fwd_local, 0)

    def fwd_mate(h, carry):
        t, par = h // 2, h % 2
        o2 = off2(t, par)
        merge(h, o2, N64, *forward(two(qm, (par, t), o2, N64), g2[0, t], g2[1, t]))
        return carry

    for a in range(2):
        to2(a).wait_recv()
    lax.fori_loop(0, N8, fwd_mate, 0)

    colt[...] = jnp.zeros_like(colt)

    def fwd_group(h, carry):
        t, par = h // 2, h % 2
        o3 = off3(t, par)
        merge(h, o3, N32, *forward(two(qm, (par, t), o3, N32), g3[0, t], g3[1, t]))
        lt = lh[h]
        att = oh[h] / lt
        lse = mh[h] + jnp.log(lt)
        delta = jnp.broadcast_to(jnp.sum(dom[par, t].astype(F32) * att, axis=1, keepdims=True), (N512, N128))
        oh[h] = att
        lseh[h] = lse
        delh[h] = delta
        lane = lax.broadcasted_iota(jnp.int32, (N512, N128), 1)
        colt[0:N512, :] = jnp.where(lane == h, lse, jnp.where(lane == h + N8, delta, colt[0:N512, :]))
        o2 = off2(t, par)
        lane = lane[:N128]
        colt[N512:N640, :] = jnp.where(lane == h, two(lseh, (h,), o2, N64), jnp.where(lane == h + N8, two(delh, (h,), o2, N64), colt[N512:N640, :]))
        l3 = two(lseh, (h,), o3, N32)
        d3 = two(delh, (h,), o3, N32)
        l3 = jnp.concatenate([l3, l3], axis=0)
        d3 = jnp.concatenate([d3, d3], axis=0)
        colt[N640:N768, :] = jnp.where(lane == h, l3, jnp.where(lane == h + N8, d3, colt[N640:N768, :]))
        return carry

    for a in range(2):
        for d in (1, 2, 3):
            to3(a, d).wait_recv()
    lax.fori_loop(0, N8, fwd_group, 0)

    st2[0] = jnp.transpose(colt[N512:N640, :])[:N16]
    st3[0] = jnp.transpose(colt[N640:N768, :])[:N16]

    def stat2():
        return red.send(st2.at[0], st2.at[1], t2s, t2r, peers[1])

    def stat3(d):
        return red.send(st3.at[0], st3.at[d], t3s.at[d], t3r.at[d], peers[d])

    for j in range(N4):
        rowt[j] = jnp.transpose(colt[N128 * j:N128 * j + N128, :])[:N16]
    for d in (2, 3):
        stat3(d).start()
    stat2().start()
    stat3(1).start()
    for t in range(N4):
        attnb[:, N128 * t:N128 * t + N128] = jnp.where(low, oh[2 * t], oh[2 * t + 1]).astype(BF16)

    def transposed_grads(q, d_rows, k, v, lse_row, delta_row):
        pt = jnp.exp(dot(k, q, NT) - lse_row)
        dst = (pt * (dot(v, d_rows, NT) - delta_row)).astype(BF16)
        return dot(dst, q), dot(pt.astype(BF16), d_rows), dst

    def grad_q(q, d_rows, k, v, lse, delta):
        p = jnp.exp(dot(q, k, NT) - wide(lse))
        ds = (p * (dot(d_rows, v, NT) - wide(delta))).astype(BF16)
        return dot(ds, k)

    lo1 = lax.broadcasted_iota(jnp.int32, (1, N128), 1) < N64

    def wait_stats():
        stat2().wait_recv()
        for d in (1, 2, 3):
            stat3(d).wait_recv()
        for a in (2, 3):
            to2(a).wait_recv()
            for d in (1, 2, 3):
                to3(a, d).wait_recv()

    def rows2(i, j, h):
        return jnp.concatenate([rowt[i, pl.ds(h, 1), :], rowt[j, pl.ds(h, 1), :]], axis=1)

    def backward(t, par):
        h = 2 * t + par

        @pl.when(par == 0)
        def _():
            dka[...] = jnp.zeros_like(dka)
            dva[...] = jnp.zeros_like(dva)

        for s in range(2):
            rows = slice(N256 * s, N256 * s + N256)
            k = kt[t, rows, :]
            gk, gv, dst = transposed_grads(qm[par, t, rows, :], dom[par, t, rows, :], k, vt[t, rows, :], rows2(2 * s, 2 * s + 1, h), rows2(2 * s, 2 * s + 1, h + N8))
            dqh[par, rows, :] = dot(dst, k, TN)
            dka[rows, :] += gk
            dva[rows, :] += gv
        a = pl.multiple_of(N128 * par, N128)
        lr, dr = rows2(par, 2 + par, h), rows2(par, 2 + par, h + N8)
        k = two(kt, (t,), a, N128)
        gk, gv, dst = transposed_grads(two(qm, (par, t), a, N128), two(dom, (par, t), a, N128), k, two(vt, (t,), a, N128), lr, dr)
        add_two(dqh, (par,), a, N128, dot(dst, k, TN))
        add_two(dka, (), a, N128, gk)
        add_two(dva, (), a, N128, gv)

        pl.when(h == 0)(wait_stats)
        off = off2(t, par)
        q, d_rows = two(qm, (par, t), off, N64), two(dom, (par, t), off, N64)
        add_two(dqh, (par,), off, N64, grad_q(q, d_rows, g2[0, t], g2[1, t], two(lseh, (h,), off, N64), two(delh, (h,), off, N64)))
        lr = jnp.concatenate([st2[0, pl.ds(h, 1), :], st2[1, pl.ds(h, 1), :]], axis=1)
        dr = jnp.concatenate([st2[0, pl.ds(h + N8, 1), :], st2[1, pl.ds(h + N8, 1), :]], axis=1)
        gk, gv, _ = transposed_grads(g2[2, t] * keep[par, :N256, :], g2[3, t] * keep[par, :N256, :], two(kt, (t,), off, N64), two(vt, (t,), off, N64), lr, dr)
        add_two(dka, (), off, N64, gk)
        add_two(dva, (), off, N64, gv)
        off = off3(t, par)
        q, d_rows = two(qm, (par, t), off, N32), two(dom, (par, t), off, N32)
        add_two(dqh, (par,), off, N32, grad_q(q, d_rows, g3[0, t], g3[1, t], two(lseh, (h,), off, N32), two(delh, (h,), off, N32)))

        def row3(i):
            r = [st3[d, pl.ds(i, 1), :] for d in range(N4)]
            return jnp.concatenate([jnp.where(lo1, r[0], r[1]), jnp.where(lo1, r[2], r[3])], axis=1)

        gk, gv, _ = transposed_grads(g3[2, t] * keep[par, :N256, :], g3[3, t] * keep[par, :N256, :], two(kt, (t,), off, N32), two(vt, (t,), off, N32), row3(h), row3(h + N8))
        add_two(dka, (), off, N32, gk)
        add_two(dva, (), off, N32, gv)

    def chunk(t):
        cols = lanes_of(t, N128)
        dq = jnp.where(low, dqh[0], dqh[1]) * (HEAD_DIM ** -0.5)
        for i, g in enumerate((dq, dka[...], dva[...])):
            gb = g.astype(BF16)
            grads[i, :, cols] = gb
            cb[t, N512 * i:N512 * i + N512, :] = dot(xp[...], gb, TN)
        g = dot(attnb[:, cols], dyp[...], TN)
        for j in range(N4):
            cb[t, 1536 + N128 * j:1664 + N128 * j, :] = g[:, N128 * j:N128 * j + N128]

    def pair(t, carry):
        def head(par, c):
            backward(t, par)
            return c

        lax.fori_loop(0, 2, head, 0)
        chunk(t)
        red.phase(0, t)
        for i in range(1, N4):
            @pl.when(t >= i)
            def _():
                red.phase(i, t - i)
        return carry

    lax.fori_loop(0, N4, pair, 0)

    def y_part(s):
        rows = slice(N256 * s, N256 * s + N256)
        yb = dot(attnb[rows, :], wo_ref[...]).astype(BF16)
        y_buf[rows, :] = dot(perm, yb, TN).astype(BF16)

    def dx_part(s):
        rows = slice(N256 * s, N256 * s + N256)
        dxb = (dot(grads[0, rows, :], wq_ref[...], NT) + dot(grads[1, rows, :], wk_ref[...], NT) + dot(grads[2, rows, :], wv_ref[...], NT)).astype(BF16)
        dx_buf[rows, :] = dot(perm, dxb, TN).astype(BF16)

    def done(c):
        red.phase(7, c)
        for x in write_out(res, (o0, o1, o2, o3), wsem, c):
            x.start()

    y_out = pltpu.make_async_copy(y_buf, y_hbm, osem.at[0])
    dx_out = pltpu.make_async_copy(dx_buf, dx_hbm, osem.at[1])
    red.phase(1, 3)
    red.phase(2, 2)
    red.phase(3, 1)
    red.phase(N4, 0)
    dx_part(0)
    red.phase(2, 3)
    red.phase(3, 2)
    red.phase(N4, 1)
    red.phase(5, 0)
    dx_part(1)
    red.phase(3, 3)
    red.phase(N4, 2)
    red.phase(5, 1)
    y_part(0)
    red.phase(N4, 3)
    red.phase(5, 2)
    red.phase(6, 0)
    y_part(1)
    red.phase(5, 3)
    y_out.start()
    dx_out.start()
    done(0)
    red.phase(6, 1)
    red.phase(6, 2)
    done(1)
    red.phase(6, 3)
    done(2)
    done(3)

    for a in range(N4):
        to2(a).wait_send()
        for d in (1, 2, 3):
            to3(a, d).wait_send()
    stat2().wait_send()
    for d in (1, 2, 3):
        stat3(d).wait_send()

    def finish(c, carry):
        red.finish(c)
        for x in write_out(res, (o0, o1, o2, o3), wsem, c):
            x.wait()
        return carry

    lax.fori_loop(0, N4, finish, 0)
    y_out.wait()
    dx_out.wait()


def attention(x_loc, w_q, w_k, w_v, w_o, dy_loc):
    vmem = pl.BlockSpec(memory_space=pltpu.VMEM)
    sem = pltpu.SemaphoreType.DMA
    bufs, sems = reducer_scratch()
    act = pltpu.VMEM((N512, N512), BF16)
    pairs = pltpu.VMEM((N4, N512, N128), BF16)
    heads = pltpu.VMEM((N8, N512, N128), F32)
    return pl.pallas_call(
        attention_kernel,
        out_shape=[jax.ShapeDtypeStruct((N512, N512), BF16)] * 2 + [jax.ShapeDtypeStruct((N512, N512), F32)] * N4,
        in_specs=[vmem] * 6,
        out_specs=[pl.BlockSpec(memory_space=pl.ANY)] * 6,
        scratch_shapes=[
            act, act, pltpu.VMEM((2, N4, N512, N128), BF16), pairs, pairs, pltpu.VMEM((2, N4, N512, N128), BF16),
            pltpu.VMEM((N4, N4, N256, N128), BF16), pltpu.VMEM((N4, N4, N256, N128), BF16), pltpu.VMEM((2, N512, N128), BF16),
            heads, heads, heads, heads, heads,
            pltpu.VMEM((2, N512, N128), F32), pltpu.VMEM((N512, N128), F32), pltpu.VMEM((N512, N128), F32), act, pltpu.VMEM((3, N512, N512), BF16),
            pltpu.VMEM((2, N16, N128), F32), pltpu.VMEM((N4, N16, N128), F32), pltpu.VMEM((N768, N128), F32), pltpu.VMEM((N4, N16, N128), F32),
            sem((N4,)), sem((N4,)), sem((N4, N4)), sem((N4, N4)), sem, sem, sem((N4,)), sem((N4,)),
            act, act, pltpu.VMEM((N4, 2048, N128), F32),
        ] + bufs + [sem((N4, 7)), sem((2,))] + sems,
        compiler_params=pltpu.CompilerParams(collective_id=0, has_side_effects=True, vmem_limit_bytes=60 * 2 ** 20),
        name="attention_step",
    )(x_loc, w_q, w_k, w_v, w_o, dy_loc)


def solution(mesh):
    def device_step(x_loc, w_q, w_k, w_v, w_o, dy_loc):
        return tuple(attention(x_loc, w_q, w_k, w_v, w_o, dy_loc))

    row_spec = P(("dp", "sp"), None)
    full_spec = P(None, None)
    grad_spec = P("dp", None)
    return jax.shard_map(device_step, mesh=mesh, in_specs=(row_spec, full_spec, full_spec, full_spec, full_spec, row_spec),
                         out_specs=(row_spec, row_spec, grad_spec, grad_spec, grad_spec, grad_spec), check_vma=False)
```

time: 94.3 us -> 86.1 us (0.913)
  Pallas kernels: 84.8 us -> 76.6 us
    pallas_call x1, Pallas kernels: 84.8 us -> 76.6 us  [attention(): pl.pallas_call(attention_kernel, out_shape=[jax.ShapeDtypeStruct((N512, N...]
where the time goes in v3:
time: 86.1 us; the launch traced here: 85.8 us
  Pallas kernels  76.6 us (89%)
  local copies, waits for them, and re-layouts  8.56 us (10%)
    pallas_call x1, Pallas kernels, attention(): pl.pallas_call(attention_kernel, out_shape=[jax.ShapeDtypeStruct((N512, N...  76.6 us
    unnamed x16, local copies, waits for them, and re-layouts  8.56 us

profile of v3, /device:TPU:1, one launch (start us, length us, event | category | flops | bytes accessed | tf_op | source)
XLA Modules:
  0.0 85.8 jit_solution(9040636965117995316)
XLA Ops:
  0.6 76.6 %attention_step.1 = (bf16[512,512]{1,0:T(8,128)(2,1)}, bf16[512,512]{1,0:T(8,128)(2,1)}, f32[512,512]{1,0:T(8,128)}, f32[512,512]{1,0:T(8,128)}, f32[512,512]{1,0:T(8,128)}, /*index=5*/f32[512,512]{1,0:T(8,128)}) custom-call(bf16[512,512]{1,0:T(8,128)(2,1)} %x_ref.1, bf16[512,512]{1,0:T(8,128)(2,1)} %wq_ref.1, bf16[512,512]{1,0:T(8,128)(2,1)} %wk_ref.1, ...), custom_call_target="tpu_custom_call" | custom-call | tf_op jit(solution)/shard_map/attention_step/pallas_call | solution.py:561
  77.2 0.0 copy-start.4
  77.2 0.0 copy-start.3
  77.2 2.0 %copy.18 = bf16[512,512]{1,0:T(8,128)(2,1)} copy(bf16[512,512]{1,0:T(8,128)(2,1)} %get-tuple-element.12) | data formatting | bytes 1048576
  79.2 0.0 copy-done.4
  79.2 0.8 copy.19
  80.0 0.0 copy-done.3
  80.0 0.0 copy-start.2
  80.0 1.0 %copy.20 = f32[512,512]{1,0:T(8,128)} copy(f32[512,512]{1,0:T(8,128)S(1)} %copy-done.3) | data formatting | bytes 2097152
  81.0 0.6 copy-done.2
  81.6 0.0 copy-start.1
  81.6 1.0 %copy.21 = f32[512,512]{1,0:T(8,128)} copy(f32[512,512]{1,0:T(8,128)S(1)} %copy-done.2) | data formatting | bytes 2097152
  82.6 0.6 copy-done.1
  83.2 0.0 copy-start
  83.2 1.0 %copy.22 = f32[512,512]{1,0:T(8,128)} copy(f32[512,512]{1,0:T(8,128)S(1)} %copy-done.1) | data formatting | bytes 2097152
  84.2 0.6 copy-done
  84.8 1.0 %copy.23 = f32[512,512]{1,0:T(8,128)} copy(f32[512,512]{1,0:T(8,128)S(1)} %copy-done) | data formatting | bytes 2097152
Async XLA Ops:
  77.2 2.0 %copy-start.4 = (bf16[512,512]{1,0:T(8,128)(2,1)S(1)}, bf16[512,512]{1,0:T(8,128)(2,1)}, u32[]{:S(2)}) copy-start(bf16[512,512]{1,0:T(8,128)(2,1)} %get-tuple-element.13) | copy-start | bytes 1572868
  77.2 2.8 %copy-start.3 = (f32[512,512]{1,0:T(8,128)S(1)}, f32[512,512]{1,0:T(8,128)}, u32[]{:S(2)}) copy-start(f32[512,512]{1,0:T(8,128)} %get-tuple-element.14) | copy-start | bytes 3145732
  80.0 1.6 %copy-start.2 = (f32[512,512]{1,0:T(8,128)S(1)}, f32[512,512]{1,0:T(8,128)}, u32[]{:S(2)}) copy-start(f32[512,512]{1,0:T(8,128)} %get-tuple-element.15) | copy-start | bytes 3145732
  81.6 1.6 %copy-start.1 = (f32[512,512]{1,0:T(8,128)S(1)}, f32[512,512]{1,0:T(8,128)}, u32[]{:S(2)}) copy-start(f32[512,512]{1,0:T(8,128)} %get-tuple-element.16) | copy-start | bytes 3145732
  83.2 1.6 %copy-start = (f32[512,512]{1,0:T(8,128)S(1)}, f32[512,512]{1,0:T(8,128)}, u32[]{:S(2)}) copy-start(f32[512,512]{1,0:T(8,128)} %get-tuple-element.17) | copy-start | bytes 3145732

commit v4 on v3

--- a/solution.py
+++ b/solution.py
@@ -198,9 +198,9 @@
     return copies
 
 
-def attention_kernel(x_ref, wq_ref, wk_ref, wv_ref, wo_ref, dy_ref, y_hbm, dx_hbm, o0, o1, o2, o3,
-                     xp, dyp, qm, kt, vt, dom, g2, g3, keep, mh, lh, oh, lseh, delh, dqh, dka, dva, attnb, grads,
-                     st2, st3, colt, rowt, s2s, s2r, s3s, s3r, t2s, t2r, t3s, t3r, y_buf, dx_buf, cb, res, pbuf, r1, r2, r3, wsem, osem, *rsems):
+def attention_kernel(x_hbm, wq_hbm, wk_hbm, wv_hbm, wo_hbm, dy_hbm, y_buf, dx_buf, res,
+                     x_ref, wq_ref, wk_ref, wv_ref, wo_ref, dy_ref, isem, xp, dyp, qm, kt, vt, dom, g2, g3, keep, mh, lh, oh, lseh, delh, dqh, dka, dva, attnb, grads,
+                     st2, st3, colt, rowt, s2s, s2r, s3s, s3r, t2s, t2r, t3s, t3r, cb, pbuf, r1, r2, r3, *rsems):
     red = Reducer(cb, res, pbuf, r1, r2, r3, rsems)
     me = red.me
     member = me % N4
@@ -211,6 +211,11 @@
     barrier = pltpu.get_barrier_semaphore()
     for p in everyone:
         pl.semaphore_signal(barrier, inc=1, device_id={"sp": p}, device_id_type=MESH)
+
+    loads = [pltpu.make_async_copy(src, dst, isem.at[i]) for i, (src, dst) in enumerate(
+        ((x_hbm, x_ref), (wk_hbm, wk_ref), (wv_hbm, wv_ref), (dy_hbm, dy_ref), (wq_hbm, wq_ref), (wo_hbm, wo_ref)))]
+    for x in loads:
+        x.start()
 
     ri = lax.broadcasted_iota(jnp.int32, (N256, N256), 0)
     ci = lax.broadcasted_iota(jnp.int32, (N256, N256), 1)
@@ -235,6 +240,8 @@
     def rows_of(s):
         return pl.ds(pl.multiple_of(N256 * s, N256), N256)
 
+    for x in loads[:3]:
+        x.wait()
     for s in range(2):
         rows = slice(N256 * s, N256 * s + N256)
         xp[rows, :] = dot(perm, x_ref[rows, :]).astype(BF16)
@@ -273,9 +280,8 @@
                 to3(a, d).start()
             to2(a).start()
 
-    pl.semaphore_wait(barrier, len(everyone))
-    send_group((0, 1))
-
+    for x in loads[3:]:
+        x.wait()
     for s in range(2):
         rows = slice(N256 * s, N256 * s + N256)
         dyp[rows, :] = dot(perm, dy_ref[rows, :]).astype(BF16)
@@ -297,7 +303,8 @@
 
     lax.fori_loop(0, 2, project_qo, 0)
     lax.fori_loop(0, N4, pack_qo, 0)
-    send_group((2, 3))
+    pl.semaphore_wait(barrier, len(everyone))
+    send_group(range(N4))
 
     def forward(q, k, v):
         s = dot(q, k, NT)
@@ -319,59 +326,85 @@
         put_two(lh, (h,), start, n, l0 * a + l * b)
         put_two(oh, (h,), start, n, o0 * a + o * b)
 
-    def fwd_local(h, carry):
-        t, par = h // 2, h % 2
-        for s in range(2):
-            rows = slice(N256 * s, N256 * s + N256)
-            m, l, o = forward(qm[par, t, rows, :], kt[t, rows, :], vt[t, rows, :])
-            mh[h, rows, :] = m
-            lh[h, rows, :] = l
-            oh[h, rows, :] = o
-        a = pl.multiple_of(N128 * par, N128)
-        merge(h, a, N128, *forward(two(qm, (par, t), a, N128), two(kt, (t,), a, N128), two(vt, (t,), a, N128)))
-        return carry
-
-    lax.fori_loop(0, N8, fwd_local, 0)
-
-    def fwd_mate(h, carry):
-        t, par = h // 2, h % 2
-        o2 = off2(t, par)
-        merge(h, o2, N64, *forward(two(qm, (par, t), o2, N64), g2[0, t], g2[1, t]))
+    def fwd_local(t, carry):
+        got = []
+        for par in range(2):
+            segs = [forward(qm[par, t, N256 * s:N256 * s + N256, :], kt[t, N256 * s:N256 * s + N256, :], vt[t, N256 * s:N256 * s + N256, :]) for s in range(2)]
+            a = N128 * par
+            got.append((segs, forward(two(qm, (par, t), a, N128), two(kt, (t,), a, N128), two(vt, (t,), a, N128))))
+        for par in range(2):
+            h = 2 * t + par
+            segs, both = got[par]
+            for s in range(2):
+                a = N128 * par
+                m, l, o = segs[s]
+                mb, lb, ob = [v[N128 * s:N128 * s + N128] for v in both]
+                ma, la, oa = [v[a:a + N128] for v in segs[s]]
+                mn = jnp.maximum(ma, mb)
+                wa = jnp.exp(ma - mn)
+                wb = jnp.exp(mb - mn)
+                r = N256 * s + a
+                z = N256 * s + N128 - a
+                mh[h, r:r + N128, :] = mn
+                lh[h, r:r + N128, :] = la * wa + lb * wb
+                oh[h, r:r + N128, :] = oa * wa + ob * wb
+                mh[h, z:z + N128, :] = m[N128 - a:N256 - a]
+                lh[h, z:z + N128, :] = l[N128 - a:N256 - a]
+                oh[h, z:z + N128, :] = o[N128 - a:N256 - a]
+        return carry
+
+    lax.fori_loop(0, N4, fwd_local, 0)
+
+    def fwd_mate(t, carry):
+        got = [forward(two(qm, (par, t), off2(t, par), N64), g2[0, t], g2[1, t]) for par in range(2)]
+        for par in range(2):
+            merge(2 * t + par, off2(t, par), N64, *got[par])
         return carry
 
     for a in range(2):
         to2(a).wait_recv()
-    lax.fori_loop(0, N8, fwd_mate, 0)
+    lax.fori_loop(0, N4, fwd_mate, 0)
 
     colt[...] = jnp.zeros_like(colt)
 
-    def fwd_group(h, carry):
-        t, par = h // 2, h % 2
-        o3 = off3(t, par)
-        merge(h, o3, N32, *forward(two(qm, (par, t), o3, N32), g3[0, t], g3[1, t]))
-        lt = lh[h]
-        att = oh[h] / lt
-        lse = mh[h] + jnp.log(lt)
-        delta = jnp.broadcast_to(jnp.sum(dom[par, t].astype(F32) * att, axis=1, keepdims=True), (N512, N128))
-        oh[h] = att
-        lseh[h] = lse
-        delh[h] = delta
-        lane = lax.broadcasted_iota(jnp.int32, (N512, N128), 1)
-        colt[0:N512, :] = jnp.where(lane == h, lse, jnp.where(lane == h + N8, delta, colt[0:N512, :]))
-        o2 = off2(t, par)
-        lane = lane[:N128]
-        colt[N512:N640, :] = jnp.where(lane == h, two(lseh, (h,), o2, N64), jnp.where(lane == h + N8, two(delh, (h,), o2, N64), colt[N512:N640, :]))
-        l3 = two(lseh, (h,), o3, N32)
-        d3 = two(delh, (h,), o3, N32)
-        l3 = jnp.concatenate([l3, l3], axis=0)
-        d3 = jnp.concatenate([d3, d3], axis=0)
-        colt[N640:N768, :] = jnp.where(lane == h, l3, jnp.where(lane == h + N8, d3, colt[N640:N768, :]))
+    def fwd_group(t, carry):
+        got = [forward(two(qm, (par, t), off3(t, par), N32), g3[0, t], g3[1, t]) for par in range(2)]
+        for par in range(2):
+            merge(2 * t + par, off3(t, par), N32, *got[par])
+        atts, stats = [], []
+        for par in range(2):
+            h = 2 * t + par
+            lt = lh[h]
+            att = oh[h] / lt
+            lse = mh[h] + jnp.log(lt)
+            delta = jnp.broadcast_to(jnp.sum(dom[par, t].astype(F32) * att, axis=1, keepdims=True), (N512, N128))
+            atts.append(att)
+            stats.append((lse, delta))
+            lseh[h] = lse
+            delh[h] = delta
+        attnb[:, lanes_of(t, N128)] = jnp.where(low, atts[0], atts[1]).astype(BF16)
+
+        def columns(part, n, take):
+            lane = lax.broadcasted_iota(jnp.int32, (n, N128), 1)
+            val = colt[part, :]
+            for par in range(2):
+                h = 2 * t + par
+                lse, delta = take(par, h)
+                val = jnp.where(lane == h, lse, jnp.where(lane == h + N8, delta, val))
+            colt[part, :] = val
+
+        def twice(v):
+            return jnp.concatenate([v, v], axis=0)
+
+        columns(slice(0, N512), N512, lambda par, h: stats[par])
+        columns(slice(N512, N640), N128, lambda par, h: [two(r, (h,), off2(t, par), N64) for r in (lseh, delh)])
+        columns(slice(N640, N768), N128, lambda par, h: [twice(two(r, (h,), off3(t, par), N32)) for r in (lseh, delh)])
         return carry
 
     for a in range(2):
         for d in (1, 2, 3):
             to3(a, d).wait_recv()
-    lax.fori_loop(0, N8, fwd_group, 0)
+    lax.fori_loop(0, N4, fwd_group, 0)
 
     st2[0] = jnp.transpose(colt[N512:N640, :])[:N16]
     st3[0] = jnp.transpose(colt[N640:N768, :])[:N16]
@@ -388,8 +421,6 @@
         stat3(d).start()
     stat2().start()
     stat3(1).start()
-    for t in range(N4):
-        attnb[:, N128 * t:N128 * t + N128] = jnp.where(low, oh[2 * t], oh[2 * t + 1]).astype(BF16)
 
     def transposed_grads(q, d_rows, k, v, lse_row, delta_row):
         pt = jnp.exp(dot(k, q, NT) - lse_row)
@@ -415,54 +446,54 @@
     def rows2(i, j, h):
         return jnp.concatenate([rowt[i, pl.ds(h, 1), :], rowt[j, pl.ds(h, 1), :]], axis=1)
 
-    def backward(t, par):
-        h = 2 * t + par
-
-        @pl.when(par == 0)
-        def _():
-            dka[...] = jnp.zeros_like(dka)
-            dva[...] = jnp.zeros_like(dva)
-
-        for s in range(2):
-            rows = slice(N256 * s, N256 * s + N256)
-            k = kt[t, rows, :]
-            gk, gv, dst = transposed_grads(qm[par, t, rows, :], dom[par, t, rows, :], k, vt[t, rows, :], rows2(2 * s, 2 * s + 1, h), rows2(2 * s, 2 * s + 1, h + N8))
-            dqh[par, rows, :] = dot(dst, k, TN)
-            dka[rows, :] += gk
-            dva[rows, :] += gv
-        a = pl.multiple_of(N128 * par, N128)
-        lr, dr = rows2(par, 2 + par, h), rows2(par, 2 + par, h + N8)
-        k = two(kt, (t,), a, N128)
-        gk, gv, dst = transposed_grads(two(qm, (par, t), a, N128), two(dom, (par, t), a, N128), k, two(vt, (t,), a, N128), lr, dr)
-        add_two(dqh, (par,), a, N128, dot(dst, k, TN))
-        add_two(dka, (), a, N128, gk)
-        add_two(dva, (), a, N128, gv)
-
-        pl.when(h == 0)(wait_stats)
-        off = off2(t, par)
-        q, d_rows = two(qm, (par, t), off, N64), two(dom, (par, t), off, N64)
-        add_two(dqh, (par,), off, N64, grad_q(q, d_rows, g2[0, t], g2[1, t], two(lseh, (h,), off, N64), two(delh, (h,), off, N64)))
-        lr = jnp.concatenate([st2[0, pl.ds(h, 1), :], st2[1, pl.ds(h, 1), :]], axis=1)
-        dr = jnp.concatenate([st2[0, pl.ds(h + N8, 1), :], st2[1, pl.ds(h + N8, 1), :]], axis=1)
-        gk, gv, _ = transposed_grads(g2[2, t] * keep[par, :N256, :], g2[3, t] * keep[par, :N256, :], two(kt, (t,), off, N64), two(vt, (t,), off, N64), lr, dr)
-        add_two(dka, (), off, N64, gk)
-        add_two(dva, (), off, N64, gv)
-        off = off3(t, par)
-        q, d_rows = two(qm, (par, t), off, N32), two(dom, (par, t), off, N32)
-        add_two(dqh, (par,), off, N32, grad_q(q, d_rows, g3[0, t], g3[1, t], two(lseh, (h,), off, N32), two(delh, (h,), off, N32)))
-
-        def row3(i):
-            r = [st3[d, pl.ds(i, 1), :] for d in range(N4)]
-            return jnp.concatenate([jnp.where(lo1, r[0], r[1]), jnp.where(lo1, r[2], r[3])], axis=1)
-
-        gk, gv, _ = transposed_grads(g3[2, t] * keep[par, :N256, :], g3[3, t] * keep[par, :N256, :], two(kt, (t,), off, N32), two(vt, (t,), off, N32), row3(h), row3(h + N8))
-        add_two(dka, (), off, N32, gk)
-        add_two(dva, (), off, N32, gv)
+    def backward_local(t):
+        got = []
+        for par in range(2):
+            h = 2 * t + par
+            tiles = []
+            for s in range(3):
+                if s < 2:
+                    q, d_rows, k, v = [r[lead + (slice(N256 * s, N256 * s + N256), slice(0, N128))] for r, lead in ((qm, (par, t)), (dom, (par, t)), (kt, (t,)), (vt, (t,)))]
+                    i, j = 2 * s, 2 * s + 1
+                else:
+                    q, d_rows, k, v = [two(r, lead, N128 * par, N128) for r, lead in ((qm, (par, t)), (dom, (par, t)), (kt, (t,)), (vt, (t,)))]
+                    i, j = par, 2 + par
+                gk, gv, dst = transposed_grads(q, d_rows, k, v, rows2(i, j, h), rows2(i, j, h + N8))
+                tiles.append((dot(dst, k, TN), gk, gv))
+            got.append(tiles)
+        for par in range(2):
+            a = N128 * par
+            for s in range(2):
+                for ref, own, both in zip((dqh, dka, dva), got[par][s], got[par][2]):
+                    r = N256 * s + a
+                    z = N256 * s + N128 - a
+                    ref[par, r:r + N128, :] = own[a:a + N128] + both[N128 * s:N128 * s + N128]
+                    ref[par, z:z + N128, :] = own[N128 - a:N256 - a]
+
+    def row3(i):
+        r = [st3[d, pl.ds(i, 1), :] for d in range(N4)]
+        return jnp.concatenate([jnp.where(lo1, r[0], r[1]), jnp.where(lo1, r[2], r[3])], axis=1)
+
+    def row2(i):
+        return jnp.concatenate([st2[0, pl.ds(i, 1), :], st2[1, pl.ds(i, 1), :]], axis=1)
+
+    def backward_group(t):
+        got = []
+        for g, n, off, row in ((g2, N64, off2, row2), (g3, N32, off3, row3)):
+            for par in range(2):
+                h = 2 * t + par
+                r = off(t, par)
+                gq = grad_q(two(qm, (par, t), r, n), two(dom, (par, t), r, n), g[0, t], g[1, t], two(lseh, (h,), r, n), two(delh, (h,), r, n))
+                gk, gv, _ = transposed_grads(g[2, t] * keep[par, :N256, :], g[3, t] * keep[par, :N256, :], two(kt, (t,), r, n), two(vt, (t,), r, n), row(h), row(h + N8))
+                got.append((par, r, n, (gq, gk, gv)))
+        for par, r, n, vals in got:
+            for ref, val in zip((dqh, dka, dva), vals):
+                add_two(ref, (par,), r, n, val)
 
     def chunk(t):
         cols = lanes_of(t, N128)
         dq = jnp.where(low, dqh[0], dqh[1]) * (HEAD_DIM ** -0.5)
-        for i, g in enumerate((dq, dka[...], dva[...])):
+        for i, g in enumerate((dq, dka[0] + dka[1], dva[0] + dva[1])):
             gb = g.astype(BF16)
             grads[i, :, cols] = gb
             cb[t, N512 * i:N512 * i + N512, :] = dot(xp[...], gb, TN)
@@ -471,11 +502,9 @@
             cb[t, 1536 + N128 * j:1664 + N128 * j, :] = g[:, N128 * j:N128 * j + N128]
 
     def pair(t, carry):
-        def head(par, c):
-            backward(t, par)
-            return c
-
-        lax.fori_loop(0, 2, head, 0)
+        backward_local(t)
+        pl.when(t == 0)(wait_stats)
+        backward_group(t)
         chunk(t)
         red.phase(0, t)
         for i in range(1, N4):
@@ -498,11 +527,7 @@
 
     def done(c):
         red.phase(7, c)
-        for x in write_out(res, (o0, o1, o2, o3), wsem, c):
-            x.start()
-
-    y_out = pltpu.make_async_copy(y_buf, y_hbm, osem.at[0])
-    dx_out = pltpu.make_async_copy(dx_buf, dx_hbm, osem.at[1])
+
     red.phase(1, 3)
     red.phase(2, 2)
     red.phase(3, 1)
@@ -522,8 +547,6 @@
     red.phase(6, 0)
     y_part(1)
     red.phase(5, 3)
-    y_out.start()
-    dx_out.start()
     done(0)
     red.phase(6, 1)
     red.phase(6, 2)
@@ -542,39 +565,56 @@
 
     def finish(c, carry):
         red.finish(c)
-        for x in write_out(res, (o0, o1, o2, o3), wsem, c):
-            x.wait()
         return carry
 
     lax.fori_loop(0, N4, finish, 0)
-    y_out.wait()
-    dx_out.wait()
+
+
+def write_kernel(y_buf, dx_buf, res, y_hbm, dx_hbm, o0, o1, o2, o3, wsem, osem):
+    copies = [pltpu.make_async_copy(y_buf, y_hbm, osem.at[0]), pltpu.make_async_copy(dx_buf, dx_hbm, osem.at[1])]
+    for t in range(N4):
+        copies += write_out(res, (o0, o1, o2, o3), wsem, t)
+    for x in copies:
+        x.start()
+    for x in copies:
+        x.wait()
 
 
 def attention(x_loc, w_q, w_k, w_v, w_o, dy_loc):
     vmem = pl.BlockSpec(memory_space=pltpu.VMEM)
+    hbm = pl.BlockSpec(memory_space=pltpu.HBM)
     sem = pltpu.SemaphoreType.DMA
     bufs, sems = reducer_scratch()
     act = pltpu.VMEM((N512, N512), BF16)
     pairs = pltpu.VMEM((N4, N512, N128), BF16)
     heads = pltpu.VMEM((N8, N512, N128), F32)
-    return pl.pallas_call(
+    grad = pltpu.VMEM((2, N512, N128), F32)
+    inner = pl.pallas_call(
         attention_kernel,
-        out_shape=[jax.ShapeDtypeStruct((N512, N512), BF16)] * 2 + [jax.ShapeDtypeStruct((N512, N512), F32)] * N4,
-        in_specs=[vmem] * 6,
-        out_specs=[pl.BlockSpec(memory_space=pl.ANY)] * 6,
-        scratch_shapes=[
+        out_shape=[act, act, bufs[0]],
+        in_specs=[hbm] * 6,
+        out_specs=[vmem] * 3,
+        scratch_shapes=[act] * 6 + [sem((6,)),
             act, act, pltpu.VMEM((2, N4, N512, N128), BF16), pairs, pairs, pltpu.VMEM((2, N4, N512, N128), BF16),
             pltpu.VMEM((N4, N4, N256, N128), BF16), pltpu.VMEM((N4, N4, N256, N128), BF16), pltpu.VMEM((2, N512, N128), BF16),
             heads, heads, heads, heads, heads,
-            pltpu.VMEM((2, N512, N128), F32), pltpu.VMEM((N512, N128), F32), pltpu.VMEM((N512, N128), F32), act, pltpu.VMEM((3, N512, N512), BF16),
+            grad, grad, grad, act, pltpu.VMEM((3, N512, N512), BF16),
             pltpu.VMEM((2, N16, N128), F32), pltpu.VMEM((N4, N16, N128), F32), pltpu.VMEM((N768, N128), F32), pltpu.VMEM((N4, N16, N128), F32),
             sem((N4,)), sem((N4,)), sem((N4, N4)), sem((N4, N4)), sem, sem, sem((N4,)), sem((N4,)),
-            act, act, pltpu.VMEM((N4, 2048, N128), F32),
-        ] + bufs + [sem((N4, 7)), sem((2,))] + sems,
-        compiler_params=pltpu.CompilerParams(collective_id=0, has_side_effects=True, vmem_limit_bytes=60 * 2 ** 20),
+            pltpu.VMEM((N4, 2048, N128), F32),
+        ] + bufs[1:] + sems,
+        compiler_params=pltpu.CompilerParams(collective_id=0, has_side_effects=True, vmem_limit_bytes=58 * 2 ** 20),
         name="attention_step",
     )(x_loc, w_q, w_k, w_v, w_o, dy_loc)
+    return pl.pallas_call(
+        write_kernel,
+        out_shape=[jax.ShapeDtypeStruct((N512, N512), BF16)] * 2 + [jax.ShapeDtypeStruct((N512, N512), F32)] * N4,
+        in_specs=[vmem] * 3,
+        out_specs=[hbm] * 6,
+        scratch_shapes=[sem((N4, 7)), sem((2,))],
+        compiler_params=pltpu.CompilerParams(vmem_limit_bytes=N8 * 2 ** 20),
+        name="write_results",
+    )(*inner)
 
 
 def solution(mesh):

time: 86.1 us -> 72.9 us (0.85)
  local copies, waits for them, and re-layouts: 8.56 us -> 0 us
  Pallas kernels: 76.6 us -> 72.2 us
    unnamed x16 -> x0, local copies, waits for them, and re-layouts: 8.56 us -> none
    pallas_call x1 -> x2, Pallas kernels: 76.6 us -> 72.2 us  [the longest x1 69.5 us: attention(): pl.pallas_call(attention_kernel, out_shape=[act, act, bufs[0]], in_specs=...]
where the time goes in v4:
time: 72.9 us; the launch traced here: 72.8 us
  Pallas kernels  72.2 us (99%)
    pallas_call x1, Pallas kernels, attention(): pl.pallas_call(attention_kernel, out_shape=[act, act, bufs[0]], in_specs=...  69.5 us
    pallas_call x1, Pallas kernels, attention(): pl.pallas_call(write_kernel, out_shape=[jax.ShapeDtypeStruct((N512, N512)...  2.63 us

profile of v4, /device:TPU:1, one launch (start us, length us, event | category | flops | bytes accessed | tf_op | source)
XLA Modules:
  0.0 72.8 jit_solution(10278486534647860306)
XLA Ops:
  0.6 69.5 %attention_step.1 = (bf16[512,512]{1,0:T(8,128)(2,1)S(1)}, bf16[512,512]{1,0:T(8,128)(2,1)S(1)}, f32[4,2048,128]{2,1,0:T(8,128)S(1)}) custom-call(bf16[512,512]{1,0:T(8,128)(2,1)} %x_hbm.1, bf16[512,512]{1,0:T(8,128)(2,1)} %wq_hbm.1, bf16[512,512]{1,0:T(8,128)(2,1)} %wk_hbm.1, bf16[512,512]{1,0:T(8,128)(2,1)} %wv_hbm.1, bf16[512,512]{1,0:T(8,128)(2,1)} %wo_hbm.1, ...), custom_call_target="tpu_custom_call" | custom-call | tf_op jit(solution)/shard_map/attention_step/pallas_call | solution.py:592
  70.2 2.6 %write_results.1 = (bf16[512,512]{1,0:T(8,128)(2,1)}, bf16[512,512]{1,0:T(8,128)(2,1)}, f32[512,512]{1,0:T(8,128)}, f32[512,512]{1,0:T(8,128)}, f32[512,512]{1,0:T(8,128)}, /*index=5*/f32[512,512]{1,0:T(8,128)}) custom-call(bf16[512,512]{1,0:T(8,128)(2,1)S(1)} %get-tuple-element.9.y_buf, bf16[512,512]{1,0:T(8,128)(2,1)S(1)} %get-tuple-element.10.dx_buf, ...), custom_call_target="tpu_custom_call" | custom-call | tf_op jit(solution)/shard_map/write_results/pallas_call | solution.py:609
